TPU v7x, 32 devices: a whole 2x2x4 slice. The times are simulated.
32 devices in a mesh: ctx: 8 (over y, x, core), head: 4 (over z).
Axes of the slice: x: 2, y: 2, z: 4, core: 2. Of those that a mesh axis runs over, the one named last changes fastest.
Arguments:
- tokens: bfloat16 [4096, 5376], P('ctx'), may hold values from -16 to 16
- norm_gain: bfloat16 [5376], replicated, may hold values from 0.099609375 to 1.8984375
- w_query: bfloat16 [5376, 4096], P(None, 'head'), may hold values from -4 to 4
- w_key: bfloat16 [5376, 2048], P(None, 'head'), may hold values from -1 to 1
- value_weight: bfloat16 [5376, 2048], P(None, 'head'), may hold values from -0.078125 to 0.078125
- w_out: bfloat16 [4096, 5376], P('head'), may hold values from -0.09375 to 0.09375
- mask_logit: float32 [32], P('head'), may hold values from -2 to 2
- noise_draw: float32 [32], P('head'), may hold values from 0.02 to 0.98
- cotangent: bfloat16 [4096, 5376], P('ctx'), may hold values from -16 to 16
Outputs:
- layer_out: bfloat16 [4096, 5376], P('ctx', 'head')
- grad_logit: float32 [32], P('head')
- grad_out_proj: float32 [4096, 5376], P('head', 'ctx')
All inputs are finite; a program needn't handle non-finite values.
Results may differ from a plain program's by a relative error of at most 0.025.
Values may be sent and summed in bfloat16 or wider, within the bound.
No kernel may reach another device: no remote copies, remote signals or barrier semaphores. Data moves between devices by JAX's collectives and lax.ppermute only.
A program may use at most 128 MiB of HBM per device.

v0:
```python
import math

import jax
import jax.numpy as jnp
from jax import lax
from jax.sharding import PartitionSpec as P

HEAD_SIZE = 128
WINDOW_TOKENS = 1024


EPSILON = 1e-06
BETA = 2.0 / 3.0
GAMMA = -0.1
ZETA = 1.1
PENALTY = 0.1
SCORE_SCALE = 168.0 ** (-0.5)
TRANSPOSED = (((0,), (0,)), ((), ()))


def shifted_2(value, axis, steps):
    count = lax.axis_size(axis)
    first, last = (max(0, -steps), min(count, count - steps))
    return lax.ppermute(value, axis, [(source, source + steps) for source in range(first, last)])


def hard_concrete(mask_logit, noise_draw):
    stretched = jax.nn.sigmoid(
        (jnp.log(noise_draw) - jnp.log(1.0 - noise_draw) + mask_logit) / BETA
    )
    shifted = stretched * (ZETA - GAMMA) + GAMMA
    gate_value = jnp.clip(shifted, 0.0, 1.0)
    inside = jnp.logical_and(shifted > 0.0, shifted < 1.0)
    gate_slope = jnp.where(inside, (ZETA - GAMMA) * stretched * (1.0 - stretched) / BETA, 0.0)
    expected = jax.nn.sigmoid(mask_logit - BETA * math.log(-GAMMA / ZETA))
    return (gate_value, gate_slope, PENALTY * expected * (1.0 - expected))


def body(tokens, norm_gain, w_query, w_key, value_weight, w_out, mask_logit, noise_draw, cotangent):
    tok_rows = tokens.shape[0]
    local_heads = mask_logit.shape[0]
    local_kv = w_key.shape[1] // HEAD_SIZE
    group_count_heads = local_heads // local_kv
    context = lax.axis_size("ctx")
    position = lax.axis_index("ctx")
    inv_root = 1.0 / math.sqrt(tok_rows * context)
    widened = tokens.astype(jnp.float32)
    moment = jnp.mean(jnp.square(widened), axis=1, keepdims=True)
    normed = (
        widened * lax.rsqrt(moment + EPSILON) * norm_gain.astype(jnp.float32)[None, :]
    ).astype(jnp.bfloat16)
    query_rows = jnp.dot(normed, w_query, preferred_element_type=jnp.float32).astype(jnp.bfloat16)
    rows_of_keys = jnp.dot(normed, w_key, preferred_element_type=jnp.float32).astype(jnp.bfloat16)
    rows_of_values = jnp.dot(normed, value_weight, preferred_element_type=jnp.float32).astype(
        jnp.bfloat16
    )
    reach = -(-WINDOW_TOKENS // tok_rows)
    earlier = []
    for distance in range(reach, 0, -1):
        earlier.append(shifted_2((rows_of_keys, rows_of_values), "ctx", distance))
    all_keys = jnp.concatenate([pair[0] for pair in earlier] + [rows_of_keys], axis=0)
    all_values = jnp.concatenate([pair[1] for pair in earlier] + [rows_of_values], axis=0)
    key_count = all_keys.shape[0]
    query_heads = query_rows.reshape(tok_rows, local_kv, group_count_heads, HEAD_SIZE)
    key_heads = all_keys.reshape(key_count, local_kv, HEAD_SIZE)
    value_heads = all_values.reshape(key_count, local_kv, HEAD_SIZE)
    scores = (
        jnp.einsum("rkgd,lkd->kgrl", query_heads, key_heads, preferred_element_type=jnp.float32)
        * SCORE_SCALE
    )
    query_pos = position * tok_rows + jnp.arange(tok_rows, dtype=jnp.int32)[:, None]
    key_pos = (position - reach) * tok_rows + jnp.arange(key_count, dtype=jnp.int32)[None, :]
    allowed = (key_pos <= query_pos) & (query_pos - key_pos < WINDOW_TOKENS) & (key_pos >= 0)
    scores = jnp.where(allowed, scores, -jnp.inf)
    row_max = jnp.max(scores, axis=-1, keepdims=True)
    lifted = jnp.exp(scores - row_max)
    prob_rows = (lifted / jnp.sum(lifted, axis=-1, keepdims=True)).astype(jnp.bfloat16)
    attended = jnp.einsum(
        "kgrl,lkd->rkgd", prob_rows, value_heads, preferred_element_type=jnp.float32
    )
    attended = attended.astype(jnp.bfloat16).reshape(tok_rows, local_heads * HEAD_SIZE)
    gate_value, gate_slope, penalty_term = hard_concrete(mask_logit, noise_draw)
    gate_columns = jnp.repeat(gate_value, HEAD_SIZE)
    gated = (attended.astype(jnp.float32) * gate_columns[None, :]).astype(jnp.bfloat16)
    partial_out = jnp.dot(gated, w_out, preferred_element_type=jnp.float32)
    layer_out = lax.psum_scatter(
        partial_out.astype(jnp.bfloat16), "head", scatter_dimension=1, tiled=True
    )
    columns = lax.all_to_all(cotangent, "ctx", split_axis=1, concat_axis=0, tiled=True)
    summed = lax.dot_general(
        lax.all_gather(attended, "ctx", axis=0, tiled=True),
        columns,
        TRANSPOSED,
        preferred_element_type=jnp.float32,
    )
    grad_out_proj = summed * gate_columns[:, None] * inv_root
    through = lax.dot_general(
        cotangent, w_out, (((1,), (1,)), ((), ())), preferred_element_type=jnp.float32
    )
    head_terms = jnp.sum(
        (through * attended.astype(jnp.float32)).reshape(tok_rows, local_heads, HEAD_SIZE),
        axis=(0, 2),
    )
    gate_product = lax.psum(head_terms, "ctx")
    grad_logit = gate_product * inv_root * gate_slope + penalty_term
    return (layer_out, grad_logit, grad_out_proj)


def solution(mesh):
    return jax.shard_map(
        body,
        mesh=mesh,
        in_specs=(
            P("ctx", None),
            P(),
            P(None, "head"),
            P(None, "head"),
            P(None, "head"),
            P("head", None),
            P("head"),
            P("head"),
            P("ctx", None),
        ),
        out_specs=(P("ctx", "head"), P("head"), P("head", "ctx")),
        check_vma=False,
    )
```

profile of v0, /device:TPU:0, one launch (start us, length us, event | category | flops | bytes accessed | tf_op | source)
XLA Modules:
  0.0 237.4 jit_solution(3631726317654641986)
XLA Ops:
  8.1 0.9 convert_element_type.38
  8.9 4.1 %fusion.6 = f32[512]{0:T(512)S(1)} fusion(bf16[512,5376]{1,0:T(8,128)(2,1)} %param.9), kind=kLoop, calls=%fused_computation.11 | loop fusion | flops 8257024 | bytes 5507072 | tf_op jit(solution)/shard_map/reduce_sum | solution.py:48
  13.1 5.8 %convolution_convert_fusion.2 = bf16[512,512]{1,0:T(8,128)(2,1)S(1)} fusion(bf16[5376,512]{1,0:T(8,128)(2,1)} %param.12, bf16[512,5376]{1,0:T(8,128)(2,1)S(1)} %copy-done, f32[5376]{0:T(1024)S(1)} %convert_element_type.38, f32[512]{0:T(512)S(1)} %add_rsqrt_fusion), kind=kOutput, calls=%fused_computation.31 | convolution fusion | flops 2829844480 | bytes 11557888 | tf_op jit(solution)/shard_map/dot_general | solution.py:53
  18.8 4.9 %collective-permute-start.2 = (bf16[512,512]{1,0:T(8,128)(2,1)S(1)}, bf16[512,512]{1,0:T(8,128)(2,1)S(1)}, u32[]{:S(2)}, u32[]{:S(2)}) collective-permute-start(bf16[512,512]{1,0:T(8,128)(2,1)S(1)} %convolution_convert_fusion.2), channel_id=1, source_target_pairs={{0,8},{4,12},{8,16},{12,20},{16,24},{20,28},{1,9},{5,13},{9,17},{1... | collective-permute-start | bytes 1572872 | tf_op jit(solution)/shard_map/ppermute | solution.py:24
  23.8 2.3 collective-permute-start.3
  26.0 3.8 %convolution_convert_fusion.3 = bf16[512,512]{1,0:T(8,128)(2,1)} fusion(bf16[5376,512]{1,0:T(8,128)(2,1)S(1)} %bitcast.48, bf16[512,5376]{1,0:T(8,128)(2,1)S(1)} %copy-done, f32[5376]{0:T(1024)S(1)} %convert_element_type.38, f32[512]{0:T(512)S(1)} %add_rsqrt_fusion), kind=kOutput, calls=%fused_computation.32 | convolution fusion | flops 2829844480 | bytes 11557888 | tf_op jit(solution)/shard_map/dot_general | solution.py:54
  29.9 3.9 %collective-permute-start = (bf16[512,512]{1,0:T(8,128)(2,1)}, bf16[512,512]{1,0:T(8,128)(2,1)}, u32[]{:S(2)}, u32[]{:S(2)}) collective-permute-start(bf16[512,512]{1,0:T(8,128)(2,1)} %convolution_convert_fusion.3), channel_id=1, source_target_pairs={{0,8},{4,12},{8,16},{12,20},{16,24},{20,28},{1,9},{5,13},{9,17},{1... | collective-permute-start | bytes 1572872 | tf_op jit(solution)/shard_map/ppermute | solution.py:24
  33.7 4.0 %collective-permute-start.1 = (bf16[512,512]{1,0:T(8,128)(2,1)}, bf16[512,512]{1,0:T(8,128)(2,1)}, u32[]{:S(2)}, u32[]{:S(2)}) collective-permute-start(bf16[512,512]{1,0:T(8,128)(2,1)} %convolution_convert_fusion.3), channel_id=1, source_target_pairs={{0,4},{4,8},{8,12},{12,16},{16,20},{20,24},{24,28},{1,5},{5,9},{9,... | collective-permute-start | bytes 1572872 | tf_op jit(solution)/shard_map/ppermute | solution.py:24
  37.8 10.3 %convolution_convert_fusion.1 = bf16[512,1024]{1,0:T(8,128)(2,1)S(1)} fusion(bf16[5376,1024]{1,0:T(8,128)(2,1)} %param.11, bf16[512,5376]{1,0:T(8,128)(2,1)} %param.9, f32[5376]{0:T(1024)S(1)} %convert_element_type.38, f32[512]{0:T(512)S(1)} %add_rsqrt_fusion), kind=kOutput, calls=%fused_computation.27 | convolution fusion | flops 5648678912 | bytes 17587200 | tf_op jit(solution)/shard_map/dot_general | solution.py:52
  48.1 1.5 reshape.51
  49.7 1.9 fusion.12
  51.6 0.8 copy-done.2
  52.4 1.3 pad_maximum_fusion.1
  53.7 0.4 reshape.50
  54.2 9.7 %fusion.35 = f32[4,2,512]{2,1,0:T(2,128)S(1)} fusion(pred[512,1536]{0,1:T(8,128)(4,1)} %fusion.12, bf16[1536,4,128,1]{2,1,0,3:T(4,128)(2,1)S(1)} %bitcast.41, bf16[512,4,2,128]{3,2,1,0:T(2,128)(2,1)} %reshape.51), kind=kOutput, calls=%fused_computation.51 | convolution fusion | flops 1635780096 | bytes 3424256 | tf_op jit(solution)/shard_map/sub | solution.py:76
  63.8 11.8 %fusion.18 = f32[4,1536,512,2]{2,1,3,0:T(8,128)} fusion(bf16[1536,4,128,1]{2,1,0,3:T(4,128)(2,1)S(1)} %bitcast.42, bf16[512,4,2,128]{3,2,1,0:T(2,128)(2,1)S(1)} %copy-done.1), kind=kOutput, calls=%fused_computation.29 | convolution fusion | flops 1610612736 | bytes 27787264 | tf_op jit(solution)/shard_map/rkgd,lkd->kgrl/dot_general | solution.py:68
  75.6 1.5 pad_maximum_fusion
  77.1 0.7 copy.34
  77.8 14.2 %fusion.15 = bf16[4,128,2,512]{3,1,2,0:T(8,128)(2,1)} fusion(bf16[1536,4,128,1]{0,2,3,1:T(8,128)(2,1)S(1)} %bitcast.46, f32[4,2,512]{2,1,0:T(2,128)S(1)} %fusion.35, f32[4,1536,512,2]{2,1,3,0:T(8,128)} %fusion.18, pred[512,1536]{0,1:T(8,128)(4,1)} %fusion.12), kind=kOutput, calls=%fused_computation.26 | convolution fusion | flops 1642599936 | bytes 28590080 | tf_op jit(solution)/shard_map/kgrl,lkd->rkgd/dot_general | solution.py:78
  92.0 0.0 reduce-scatter.2.cloned.1.call-start
  92.1 1.5 copy.28
  93.6 10.3 %fusion.14 = f32[1024]{0:T(1024)S(1)} fusion(bf16[512,1024]{1,0:T(8,128)(2,1)S(1)} %copy.28, bf16[512,5376]{1,0:T(8,128)(2,1)} %param.17, bf16[1024,5376]{1,0:T(8,128)(2,1)} %param.14), kind=kOutput, calls=%fused_computation.23 | convolution fusion | flops 5638716416 | bytes 17567744 | tf_op jit(solution)/shard_map/dot_general | solution.py:97
  103.9 0.1 bitcast_reduce_fusion
  104.0 12.1 %psum.7 = f32[8]{0:T(128)S(1)} all-reduce(f32[8]{0:T(128)S(1)} %bitcast_reduce_fusion), channel_id=1, replica_groups=mesh['ctx'=8,'head'=4] {'ctx'}, use_global_device_ids=true, to_apply=%region_6.7 | all-reduce | flops 8 | bytes 64 | tf_op jit(solution)/shard_map/psum | solution.py:104
  116.2 0.5 multiply_add_fusion
  116.7 0.1 broadcast_bitcast_fusion
  116.8 15.7 %convolution_convert_fusion = bf16[512,5376]{0,1:T(8,128)(2,1)} fusion(bf16[1024,5376]{1,0:T(8,128)(2,1)} %param.14, bf16[512,1024]{1,0:T(8,128)(2,1)S(1)} %copy.28, f32[1024]{0:T(1024)S(1)} %broadcast_bitcast_fusion), kind=kOutput, calls=%fused_computation.14 | convolution fusion | flops 5641469952 | bytes 17567744 | tf_op jit(solution)/shard_map/dot_general | solution.py:85
  132.5 8.4 %copy.29 = bf16[512,5376]{0,1:T(8,128)(2,1)} copy(bf16[512,5376]{1,0:T(8,128)(2,1)} %param.17) | data formatting | bytes 11010048 | tf_op args[8]
  140.9 66.7 %all_to_all.19 = bf16[512,8,672]{0,2,1:T(8,128)(2,1)S(1)} all-to-all(bf16[512,8,672]{0,2,1:T(8,128)(2,1)} %bitcast.40), channel_id=1, replica_groups=mesh['ctx'=8,'head'=4] {'ctx'}, dimensions={1} | all-to-all | bytes 11010048 | tf_op jit(solution)/shard_map/all_to_all | solution.py:89
  207.6 3.0 %copy.37 = bf16[8,84,8,512]{3,2,0,1:T(8,128)(2,1)} copy(bf16[8,84,8,512]{3,2,1,0:T(8,128)(2,1)S(1)} %bitcast.39) | data formatting | bytes 11010048 | tf_op jit(solution)/shard_map/all_to_all | solution.py:89
  210.6 11.4 %multiply_multiply_fusion = f32[1024,672]{0,1:T(8,128)} fusion(bf16[4096,1024]{0,1:T(8,128)(2,1)} %all-gather.2.cloned.1.call-done, bf16[4096,672]{0,1:T(8,128)(2,1)} %bitcast.43, f32[1024]{0:T(1024)S(1)} %broadcast_bitcast_fusion), kind=kOutput, calls=%fused_computation.19 | convolution fusion | flops 5638520832 | bytes 16650240 | tf_op jit(solution)/shard_map/dot_general | solution.py:90
  222.0 7.9 %reduce-scatter.2.cloned.1.call-done = bf16[512,1344]{0,1:T(8,128)(2,1)} async-done(((bf16[512,5376]{0,1:T(8,128)(2,1)}), bf16[512,1344]{0,1:T(8,128)(2,1)}) %reduce-scatter.2.cloned.1.call-update) | async-done | bytes 1376272 | tf_op jit(solution)/shard_map/reduce_scatter | solution.py:86
  (27 shorter events, 0.1 us)
Async XLA Ops:
  8.0 202.6 %all-gather.2.cloned.1.call-start = ((), (), s32[]{:S(2)}) async-start(), calls=%async_computation.3 | async-start | bytes 9437184 | tf_op jit(solution)/shard_map/all_gather | solution.py:91
  8.0 5.0 %copy-start = (bf16[512,5376]{1,0:T(8,128)(2,1)S(1)}, bf16[512,5376]{1,0:T(8,128)(2,1)}, u32[]{:S(2)}) copy-start(bf16[512,5376]{1,0:T(8,128)(2,1)} %param.9) | copy-start | bytes 16515076
  8.9 17.1 %slice-start = ((s8[5505024]{0:T(1024)(128)(4,1)}), s8[1310720]{0:T(1024)(128)(4,1)S(1)}, s32[]{:S(2)}) async-start(s8[5505024]{0:T(1024)(128)(4,1)} %bitcast.47), calls=%async_computation.4 | async-start | bytes 2621440
  13.1 13.0 %slice-start.1 = ((s8[5505024]{0:T(1024)(128)(4,1)}), s8[4194304]{0:T(1024)(128)(4,1)S(1)}, s32[]{:S(2)}) async-start(s8[5505024]{0:T(1024)(128)(4,1)} %bitcast.47), calls=%async_computation.5 | async-start | bytes 8388608
  18.8 32.8 %collective-permute-start.2 = (bf16[512,512]{1,0:T(8,128)(2,1)S(1)}, bf16[512,512]{1,0:T(8,128)(2,1)S(1)}, u32[]{:S(2)}, u32[]{:S(2)}) collective-permute-start(bf16[512,512]{1,0:T(8,128)(2,1)S(1)} %convolution_convert_fusion.2), channel_id=1, source_target_pairs={{0,8},{4,12},{8,16},{12,20},{16,24},{20,28},{1,9},{5,13},{9,17},{1... | collective-permute-start | bytes 1572872 | tf_op jit(solution)/shard_map/ppermute | solution.py:24
  23.8 28.7 %collective-permute-start.3 = (bf16[512,512]{1,0:T(8,128)(2,1)S(1)}, bf16[512,512]{1,0:T(8,128)(2,1)}, u32[]{:S(2)}, u32[]{:S(2)}) collective-permute-start(bf16[512,512]{1,0:T(8,128)(2,1)S(1)} %convolution_convert_fusion.2), channel_id=1, source_target_pairs={{0,4},{4,8},{8,12},{12,16},{16,20},{20,24},{24,28},{1,5},{5,9},{9,... | collective-permute-start | bytes 1572872 | tf_op jit(solution)/shard_map/ppermute | solution.py:24
  29.9 45.7 %collective-permute-start = (bf16[512,512]{1,0:T(8,128)(2,1)}, bf16[512,512]{1,0:T(8,128)(2,1)}, u32[]{:S(2)}, u32[]{:S(2)}) collective-permute-start(bf16[512,512]{1,0:T(8,128)(2,1)} %convolution_convert_fusion.3), channel_id=1, source_target_pairs={{0,8},{4,12},{8,16},{12,20},{16,24},{20,28},{1,9},{5,13},{9,17},{1... | collective-permute-start | bytes 1572872 | tf_op jit(solution)/shard_map/ppermute | solution.py:24
  33.7 41.9 %collective-permute-start.1 = (bf16[512,512]{1,0:T(8,128)(2,1)}, bf16[512,512]{1,0:T(8,128)(2,1)}, u32[]{:S(2)}, u32[]{:S(2)}) collective-permute-start(bf16[512,512]{1,0:T(8,128)(2,1)} %convolution_convert_fusion.3), channel_id=1, source_target_pairs={{0,4},{4,8},{8,12},{12,16},{16,20},{20,24},{24,28},{1,5},{5,9},{9,... | collective-permute-start | bytes 1572872 | tf_op jit(solution)/shard_map/ppermute | solution.py:24
  51.6 0.8 copy-start.2
  54.1 9.7 %copy-start.1 = (bf16[512,4,2,128]{3,2,1,0:T(2,128)(2,1)S(1)}, bf16[512,4,2,128]{3,2,1,0:T(2,128)(2,1)}, u32[]{:S(2)}) copy-start(bf16[512,4,2,128]{3,2,1,0:T(2,128)(2,1)} %reshape.51) | copy-start | bytes 3145732
  92.0 137.9 %reduce-scatter.2.cloned.1.call-start = ((), (), s32[]{:S(2)}) async-start(), calls=%async_computation.2 | async-start | bytes 6881280 | tf_op jit(solution)/shard_map/reduce_scatter | solution.py:86
  93.6 22.6 %copy-start.3 = (f32[8]{0:T(128)S(1)}, f32[8]{0:T(128)}, u32[]{:S(2)}) copy-start(f32[8]{0:T(128)} %param.15) | copy-start | bytes 100
  93.6 22.6 %copy-start.4 = (f32[8]{0:T(128)S(1)}, f32[8]{0:T(128)}, u32[]{:S(2)}) copy-start(f32[8]{0:T(128)} %param.16) | copy-start | bytes 100
Sparse Core Ops, SparseCore 0:
  92.1 56.3 all-gather.1
Sparse Core Ops, SparseCore 1:
  132.6 97.3 reduce-scatter.1
where the time goes:
time: 238 us; the launch traced here: 237 us
  matrix products  93 us (39%)
  blocking collectives  78.9 us (33%)
  local copies, waits for them, and re-layouts  16.5 us (7%)
  between operations  15.6 us (7%)
  starting transfers between devices  15.1 us (6%)
  other arithmetic  10.3 us (4%)
  waiting for transfers between devices  7.92 us (3%)
    all_to_all x1, blocking collectives, body(): lax.all_to_all(cotangent, 'ctx', split_axis=1, concat_axis=0, tiled=True)  66.7 us
    dot_general x1, matrix products, body(): partial_out = jnp.dot(gated, w_out, preferred_element_type=jnp.float32)  15.7 us
    ppermute x4, starting transfers between devices, shifted_2(): lax.ppermute(value, axis, [(source, source + steps) for source in range(f...  15.1 us
    dot_general x1, matrix products, body(): jnp.einsum('kgrl,lkd->rkgd', prob_rows, value_heads, preferred_element_ty...  14.2 us
    psum x1, blocking collectives, body(): gate_product = lax.psum(head_terms, 'ctx')  12.1 us
    dot_general x1, matrix products, body(): jnp.einsum('rkgd,lkd->kgrl', query_heads, key_heads, preferred_element_ty...  11.8 us
    dot_general x1, matrix products, body(): lax.dot_general(lax.all_gather(attended, 'ctx', axis=0, tiled=True), colu...  11.4 us
    dot_general x1, matrix products, body(): jnp.dot(normed, w_query, preferred_element_type=jnp.float32)  10.3 us
  transfers between devices with their start and end apart: 6, of which 1 were waited for; matrix products, arithmetic and copies ran while one was open for 39% of the time, Pallas kernels for 0%

commit v1 on v0

v1 whole, which is shorter than its diff:
```python
import functools
import math

import jax
import jax.numpy as jnp
from jax import lax
from jax.experimental import pallas as pl
from jax.experimental.pallas import tpu as pltpu
from jax.sharding import PartitionSpec as P


HEAD_SIZE = 128
WINDOW_TOKENS = 1024

EPSILON = 1e-06
BETA = 2.0 / 3.0
GAMMA = -0.1
ZETA = 1.1
PENALTY = 0.1
SCORE_SCALE = 168.0 ** (-0.5)
LOG2_E = 1.4426950408889634


def shift(value, axis, steps):
    count = lax.axis_size(axis)
    return lax.ppermute(value, axis, [(i, i + steps) for i in range(count - steps)])


def rotate(value, axis, steps):
    count = lax.axis_size(axis)
    return lax.ppermute(value, axis, [(i, (i + steps) % count) for i in range(count)])


def swap(value, axis, bit):
    count = lax.axis_size(axis)
    return lax.ppermute(value, axis, [(i, i ^ bit) for i in range(count)])


def hard_concrete(mask_logit, noise_draw):
    stretched = jax.nn.sigmoid(
        (jnp.log(noise_draw) - jnp.log(1.0 - noise_draw) + mask_logit) / BETA
    )
    shifted = stretched * (ZETA - GAMMA) + GAMMA
    gate_value = jnp.clip(shifted, 0.0, 1.0)
    inside = jnp.logical_and(shifted > 0.0, shifted < 1.0)
    gate_slope = jnp.where(inside, (ZETA - GAMMA) * stretched * (1.0 - stretched) / BETA, 0.0)
    expected = jax.nn.sigmoid(mask_logit - BETA * math.log(-GAMMA / ZETA))
    return (gate_value, gate_slope, PENALTY * expected * (1.0 - expected))


def after(value, *others):
    return lax.optimization_barrier((value,) + others)[0]


def attention_kernel(pos_ref, q_ref, k2_ref, k1_ref, k0_ref, v2_ref, v1_ref, v0_ref, gate_ref,
                     att_ref, gated_ref, *, block, group):
    rows = q_ref.shape[0]
    position = pos_ref[0]
    keys = (k2_ref, k1_ref, k0_ref)
    values = (v2_ref, v1_ref, v0_ref)
    bias = (
        jnp.where(position >= 2, 0.0, -jnp.inf).astype(jnp.float32),
        jnp.where(position >= 1, 0.0, -jnp.inf).astype(jnp.float32),
        None,
    )
    per = rows // block
    count = WINDOW_TOKENS // block + 1
    ones = jnp.ones((block, HEAD_SIZE), jnp.bfloat16)
    row_id = lax.broadcasted_iota(jnp.int32, (block, block), 0)
    col_id = lax.broadcasted_iota(jnp.int32, (block, block), 1)
    behind = jnp.concatenate([col_id > row_id] * group, axis=0)
    ahead = jnp.concatenate([col_id <= row_id] * group, axis=0)
    for b in range(per):
        here = pl.ds(b * block, block)
        query = jnp.concatenate(
            [q_ref[here, g * HEAD_SIZE:(g + 1) * HEAD_SIZE] for g in range(group)], axis=0
        )
        scores = []
        for s in range(count):
            piece, offset = divmod(b + s, per)
            key = keys[piece][pl.ds(offset * block, block), :]
            score = lax.dot_general(
                query, key, (((1,), (1,)), ((), ())), preferred_element_type=jnp.float32
            )
            if s == 0:
                score = jnp.where(behind, score, -jnp.inf)
            if s == count - 1:
                score = jnp.where(ahead, score, -jnp.inf)
            if bias[piece] is not None:
                score = score + bias[piece]
            scores.append(score)
        top = functools.reduce(jnp.maximum, scores)
        top = jnp.max(top, axis=1, keepdims=True)
        total = None
        for s in range(count):
            piece, offset = divmod(b + s, per)
            prob = jnp.exp2((scores[s] - top) * (SCORE_SCALE * LOG2_E)).astype(jnp.bfloat16)
            value = jnp.concatenate(
                [values[piece][pl.ds(offset * block, block), :], ones], axis=1
            )
            part = jnp.dot(prob, value, preferred_element_type=jnp.float32)
            total = part if total is None else total + part
        result = (total[:, :HEAD_SIZE] / total[:, HEAD_SIZE:]).astype(jnp.bfloat16)
        for g in range(group):
            cols = slice(g * HEAD_SIZE, (g + 1) * HEAD_SIZE)
            piece_out = result[g * block:(g + 1) * block]
            att_ref[here, cols] = piece_out
            gated_ref[here, cols] = (
                piece_out.astype(jnp.float32) * gate_ref[:, cols]
            ).astype(jnp.bfloat16)


def attention(position, queries, kv2, kv1, kv0, gate_row, side):
    rows = queries.shape[0]
    kv_heads = kv0.shape[1] // (2 * HEAD_SIZE)
    wide = queries.shape[1] // (2 * kv_heads)
    group = wide // HEAD_SIZE
    width = kv_heads * wide
    block = math.gcd(rows, 256)
    key_spec = pl.BlockSpec((rows, HEAD_SIZE), lambda h, pos: (0, h))
    value_spec = pl.BlockSpec((rows, HEAD_SIZE), lambda h, pos: (0, kv_heads + h))
    query_spec = pl.BlockSpec((rows, wide), lambda h, pos: (0, side * kv_heads + h))
    out_spec = pl.BlockSpec((rows, wide), lambda h, pos: (0, h))
    return pl.pallas_call(
        functools.partial(attention_kernel, block=block, group=group),
        grid_spec=pltpu.PrefetchScalarGridSpec(
            num_scalar_prefetch=1,
            grid=(kv_heads,),
            in_specs=[query_spec, key_spec, key_spec, key_spec, value_spec, value_spec, value_spec,
                      pl.BlockSpec((1, wide), lambda h, pos: (0, side * kv_heads + h))],
            out_specs=[out_spec, out_spec],
        ),
        out_shape=[jax.ShapeDtypeStruct((rows, width), jnp.bfloat16)] * 2,
        compiler_params=pltpu.CompilerParams(dimension_semantics=("arbitrary",)),
        cost_estimate=pl.CostEstimate(
            flops=8 * rows * (WINDOW_TOKENS + block) * width, bytes_accessed=10 * rows * width,
            transcendentals=rows * (WINDOW_TOKENS + block) * width // HEAD_SIZE),
        name="attention",
    )(position, queries, kv2, kv1, kv0, kv2, kv1, kv0, gate_row)


def terms_kernel(tab_ref, cot0_ref, cot1_ref, att0_ref, att1_ref, sent_ref, kept_ref, *, sent):
    index = pl.program_id(0)
    total = (
        jnp.dot(cot0_ref[0], att0_ref[...], preferred_element_type=jnp.float32)
        + jnp.dot(cot1_ref[0], att1_ref[...], preferred_element_type=jnp.float32)
    ).astype(jnp.bfloat16)

    @pl.when(index < sent)
    def _():
        sent_ref[0] = total

    @pl.when(index >= sent)
    def _():
        kept_ref[0] = total


def grad_terms(position, cot_blocks, cot_other, att, att_other, order):
    _, width, rows = cot_blocks.shape
    cols = att.shape[1]
    steps = len(order)
    sent = steps // 2
    owners = position ^ jnp.array(order, jnp.int32)
    table = jnp.concatenate([owners, owners // 2])
    whole = pl.BlockSpec((rows, cols), lambda j, tab: (0, 0))
    return pl.pallas_call(
        functools.partial(terms_kernel, sent=sent),
        grid_spec=pltpu.PrefetchScalarGridSpec(
            num_scalar_prefetch=1,
            grid=(steps,),
            in_specs=[
                pl.BlockSpec((1, width, rows), lambda j, tab: (tab[j], 0, 0)),
                pl.BlockSpec((1, width, rows), lambda j, tab: (tab[steps + j], 0, 0)),
                whole,
                whole,
            ],
            out_specs=[
                pl.BlockSpec((1, width, cols), lambda j, tab: (jnp.minimum(j, sent - 1), 0, 0)),
                pl.BlockSpec((1, width, cols), lambda j, tab: (jnp.maximum(j - sent, 0), 0, 0)),
            ],
        ),
        out_shape=[jax.ShapeDtypeStruct((sent, width, cols), jnp.bfloat16)] * 2,
        compiler_params=pltpu.CompilerParams(dimension_semantics=("arbitrary",)),
        cost_estimate=pl.CostEstimate(
            flops=4 * steps * width * rows * cols,
            bytes_accessed=2 * steps * width * (2 * rows + cols), transcendentals=0),
        name="grad_terms",
    )(table, cot_blocks, cot_other, att, att_other)


def project_kernel(pos_ref, *refs, turns, slots, count):
    pairs = 2 * len(turns)
    x_refs = refs[:pairs]
    rest = list(refs[pairs:])
    base_ref = rest.pop(0) if turns[0] != -1 else None
    own_ref = rest.pop(0) if turns[0] == -1 else None
    w_refs = rest[:len(slots)]
    out_ref, weight, sems = rest[len(slots):]
    position = pos_ref[0]
    copies = []
    for k, turn in enumerate(turns):
        group = []
        if turn == -1:
            group.append(pltpu.make_async_copy(own_ref, weight.at[k], sems.at[k, 0]))
        else:
            for index, relative in enumerate(slots):
                start = pl.multiple_of((position ^ relative) * count, count)
                group.append(pltpu.make_async_copy(
                    w_refs[index].at[pl.ds(turn * count, count)], weight.at[k, pl.ds(start, count)], sems.at[k, index]))
        for copy in group:
            copy.start()
        copies.append(group)
    total = None if base_ref is None else base_ref[...]
    middle = x_refs[0].shape[1]
    for k in range(len(turns)):
        for copy in copies[k]:
            copy.wait()
        for side in range(2):
            part = jnp.dot(
                x_refs[2 * k + side][...],
                weight[k, side * middle:(side + 1) * middle],
                preferred_element_type=jnp.float32,
            )
            total = part if total is None else total + part
    out_ref[...] = total[:, :out_ref.shape[1]].astype(out_ref.dtype)


def project(position, xs, base, own, weights, slots, turns, out_cols, dtype):
    rows, middle = xs[0].shape
    cols = weights[0].shape[1]
    whole = pl.BlockSpec(memory_space=pltpu.VMEM)
    anywhere = pl.BlockSpec(memory_space=pl.ANY)
    extra = [own] if base is None else [base]
    return pl.pallas_call(
        functools.partial(project_kernel, turns=turns, slots=slots, count=2 * middle // len(slots)),
        in_specs=[pl.BlockSpec(memory_space=pltpu.SMEM)] + [whole] * len(xs)
        + [anywhere if base is None else whole] + [anywhere] * len(weights),
        out_specs=whole,
        out_shape=jax.ShapeDtypeStruct((rows, out_cols), dtype),
        scratch_shapes=[
            pltpu.VMEM((len(turns), 2 * middle, cols), jnp.bfloat16),
            pltpu.SemaphoreType.DMA((len(turns), len(slots))),
        ],
        cost_estimate=pl.CostEstimate(
            flops=4 * len(turns) * rows * middle * cols,
            bytes_accessed=len(turns) * 4 * middle * (rows + cols) + 8 * rows * cols,
            transcendentals=0),
        name="project",
    )(position, *xs, *extra, *weights)


def turned_kernel(x_ref, out_ref):
    out_ref[...] = x_ref[...].T


def turned(x):
    whole = pl.BlockSpec(memory_space=pltpu.VMEM)
    return pl.pallas_call(
        turned_kernel, in_specs=[whole], out_specs=whole,
        out_shape=jax.ShapeDtypeStruct(x.shape[::-1], x.dtype), name="turned",
    )(x)


def body(tokens, norm_gain, w_query, w_key, value_weight, w_out, mask_logit, noise_draw, cotangent):
    tok_rows, model_width = tokens.shape
    local_heads = mask_logit.shape[0]
    n_ctx = lax.axis_size("ctx")
    n_head = lax.axis_size("head")
    p = lax.axis_index("ctx")
    z = lax.axis_index("head")
    position = p.astype(jnp.int32).reshape(1)
    bits = [1 << k for k in range(1, n_ctx.bit_length() - 1)]
    inv_root = 1.0 / math.sqrt(tok_rows * n_ctx)
    out_cols = model_width // n_head
    wide_cols = -(-out_cols // 128) * 128
    piece = w_out.shape[0] // n_ctx

    mine = lax.dynamic_slice_in_dim(w_out, p * piece, piece, 0)
    turns = []
    for t in range(1, n_head):
        block = lax.dynamic_slice_in_dim(mine, ((z + t) % n_head) * out_cols, out_cols, 1)
        block = jnp.pad(block, ((0, 0), (0, wide_cols - out_cols)))
        turns.append(rotate(block, "head", t))

    widened = tokens.astype(jnp.float32)
    moment = jnp.mean(jnp.square(widened), axis=1, keepdims=True)
    normed = (
        widened * lax.rsqrt(moment + EPSILON) * norm_gain.astype(jnp.float32)[None, :]
    ).astype(jnp.bfloat16)
    keys = jnp.dot(normed, w_key, preferred_element_type=jnp.float32).astype(jnp.bfloat16)
    values = jnp.dot(normed, value_weight, preferred_element_type=jnp.float32).astype(
        jnp.bfloat16)
    kv_half = keys.shape[1] // 2
    kv_sides = []
    kv2_sides = []
    for h in range(2):
        cols = slice(h * kv_half, (h + 1) * kv_half)
        kv_sides.append(jnp.concatenate([keys[:, cols], values[:, cols]], axis=1))
        kv2_sides.append(shift(kv_sides[h], "ctx", 2))
    queries = jnp.dot(
        after(normed, *kv_sides), w_query, preferred_element_type=jnp.float32
    ).astype(jnp.bfloat16)

    gate_value, gate_slope, penalty_term = hard_concrete(mask_logit, noise_draw)
    gate_columns = jnp.repeat(gate_value, HEAD_SIZE)
    gate_row = gate_columns[None, :]

    own_part = jnp.concatenate(after(tuple(turns), queries), axis=0)
    parts = {0: own_part}
    for bit in bits:
        for relative in list(parts):
            parts[relative | bit] = swap(parts[relative], "ctx", bit)

    mixed = [jnp.where(p % 2 == 0, kv_sides[h], after(kv2_sides[h], queries)) for h in range(2)]

    cot_blocks = after(cotangent, mixed[0]).T.reshape(n_ctx, model_width // n_ctx, tok_rows)
    leaving = lax.dynamic_index_in_dim(
        cot_blocks.reshape((n_ctx // 2, 2) + cot_blocks.shape[1:]), 1 - p % 2, 1, keepdims=False)
    cot_other = swap(leaving, "ctx", 1)

    attended = []
    moving = []
    others = []
    for h in range(2):
        kv1 = swap(mixed[h], "ctx", 1)
        att, gat = attention(
            position, queries, kv2_sides[h], kv1, kv_sides[h], gate_row, h)
        attended.append(att)
        chain = [gat]
        for _ in range(1, n_head):
            chain.append(rotate(chain[-1], "head", 1))
        moving.append(chain)
        others.append(swap(att, "ctx", 1))

    own_weight = jnp.pad(
        lax.dynamic_slice_in_dim(after(w_out, attended[1]), z * out_cols, out_cols, 1),
        ((0, 0), (0, wide_cols - out_cols)))

    own_cols = model_width // n_ctx
    w_mine = lax.dynamic_slice_in_dim(after(w_out, attended[1]), p * own_cols, own_cols, 1)
    w_mine = turned(jnp.pad(w_mine, ((0, 0), (0, -own_cols % 128))))[:own_cols]

    grads = []
    for h in range(2):
        steps = bits if h == 0 else bits[::-1]
        relative = [2 * j for j in range(n_ctx // 2)]
        order = [r for r in relative if r & steps[0]] + [r for r in relative if not r & steps[0]]
        sent, kept = grad_terms(
            position, cot_blocks, cot_other, attended[h], others[h], order)
        relative = order[len(order) // 2:]
        for k, bit in enumerate(steps):
            if k:
                leave = [i for i, r in enumerate(relative) if r & bit]
                stay = [i for i, r in enumerate(relative) if not r & bit]
                sent = jnp.concatenate([total[i:i + 1] for i in leave], axis=0)
                kept = jnp.concatenate([total[i:i + 1] for i in stay], axis=0)
                relative = [relative[i] for i in stay]
            received = swap(sent, "ctx", bit)
            total = kept.astype(jnp.float32) + received.astype(jnp.float32)
            if len(relative) > 1:
                total = total.astype(jnp.bfloat16)
        grads.append(total[0])

    for relative in list(parts):
        parts[relative | 1] = swap(parts[relative], "ctx", 1)
    slots = tuple(parts)
    weights = [parts[r] for r in slots]

    early = list(range(n_head - 2))
    xs = [moving[h][0] for h in range(2)]
    for t in early:
        xs += [moving[h][t + 1] for h in range(2)]
    base = project(position, xs, None, own_weight, weights, slots, (-1,) + tuple(early),
                   wide_cols, jnp.float32)
    layer_out = project(position, [moving[h][-1] for h in range(2)], base, None, weights,
                        slots, (n_head - 2,), out_cols, jnp.bfloat16)

    summed = jnp.concatenate([g.T for g in grads], axis=0)
    grad_out_proj = summed * gate_columns[:, None] * inv_root

    head_terms = jnp.sum(
        (summed.T * w_mine.astype(jnp.float32)).reshape(-1, local_heads, HEAD_SIZE), axis=(0, 2))
    for bit in [1] + bits:
        head_terms = head_terms + swap(head_terms, "ctx", bit)
    grad_logit = head_terms * inv_root * gate_slope + penalty_term
    return (layer_out, grad_logit, grad_out_proj)


def solution(mesh):
    return jax.shard_map(
        body,
        mesh=mesh,
        in_specs=(
            P("ctx", None),
            P(),
            P(None, "head"),
            P(None, "head"),
            P(None, "head"),
            P("head", None),
            P("head"),
            P("head"),
            P("ctx", None),
        ),
        out_specs=(P("ctx", "head"), P("head"), P("head", "ctx")),
        check_vma=False,
    )
```

time: 238 us -> 239 us (level)
  matrix products: 93 us -> 12.8 us
  blocking collectives: 78.9 us -> 0 us
  waiting for transfers between devices: 7.92 us -> 85.4 us
  Pallas kernels: 0 us -> 50.6 us
  starting transfers between devices: 15.1 us -> 42.7 us
  between operations: 15.6 us -> 1.15 us
  local copies, waits for them, and re-layouts: 16.5 us -> 27.2 us
  other arithmetic: 10.3 us -> 18.6 us
    ppermute x4 -> x30, waiting for transfers between devices: 0.01 us -> 85.4 us  [the longest x9 53.7 us: rotate(): lax.ppermute(value, axis, [(i, (i + steps) % count) for i in range(count)])]
    dot_general x6 -> x1, matrix products: 73.7 us -> 6.8 us  [body(): jnp.dot(after(normed, *kv_sides), w_query, preferred_element_type=jnp.flo...]
    all_to_all x1 -> x0, blocking collectives: 66.7 us -> none  [body(): lax.all_to_all(cotangent, 'ctx', split_axis=1, concat_axis=0, tiled=True)]
    pallas_call x0 -> x7, Pallas kernels: none -> 50.6 us  [the longest x2 17.7 us: project(): pl.pallas_call(functools.partial(project_kernel, turns=turns, slots=slots...]
    ppermute x4 -> x30, starting transfers between devices: 15.1 us -> 42.7 us  [the longest x9 25.5 us: rotate(): lax.ppermute(value, axis, [(i, (i + steps) % count) for i in range(count)])]
    psum x1 -> x0, blocking collectives: 12.1 us -> none  [body(): gate_product = lax.psum(head_terms, 'ctx')]
    sub x1 -> x0, matrix products: 9.66 us -> none  [body(): lifted = jnp.exp(scores - row_max)]
    optimization_barrier x0 -> x1, local copies, waits for them, and re-layouts: none -> 8.25 us  [after(): return lax.optimization_barrier((value,) + others)[0]]
  transfers between devices with their start and end apart: 6 -> 30, of which waited for: 1 -> 14; matrix products, arithmetic and copies ran while one was open for 39% -> 13% of each run, Pallas kernels for 0% -> 21%
where the time goes in v1:
time: 239 us; the launch traced here: 238 us
  waiting for transfers between devices  85.4 us (36%)
  Pallas kernels  50.6 us (21%)
  starting transfers between devices  42.7 us (18%)
  local copies, waits for them, and re-layouts  27.2 us (11%)
  other arithmetic  18.6 us (8%)
  matrix products  12.8 us (5%)
    ppermute x9, waiting for transfers between devices, rotate(): lax.ppermute(value, axis, [(i, (i + steps) % count) for i in range(count)])  53.7 us
    ppermute x9, starting transfers between devices, rotate(): lax.ppermute(value, axis, [(i, (i + steps) % count) for i in range(count)])  25.5 us
    ppermute x19, waiting for transfers between devices, swap(): return lax.ppermute(value, axis, [(i, i ^ bit) for i in range(count)])  23.6 us
    pallas_call x2, Pallas kernels, project(): pl.pallas_call(functools.partial(project_kernel, turns=turns, slots=slots...  17.7 us
    pallas_call x2, Pallas kernels, grad_terms(): pl.pallas_call(functools.partial(terms_kernel, sent=sent), grid_spec=pltp...  15.8 us
    pallas_call x2, Pallas kernels, attention(): pl.pallas_call(functools.partial(attention_kernel, block=block, group=gro...  14.1 us
    ppermute x2, starting transfers between devices, shift(): lax.ppermute(value, axis, [(i, i + steps) for i in range(count - steps)])  9.31 us
    optimization_barrier x1, local copies, waits for them, and re-layouts, after(): return lax.optimization_barrier((value,) + others)[0]  8.25 us
  transfers between devices with their start and end apart: 30, of which 14 were waited for; matrix products, arithmetic and copies ran while one was open for 13% of the time, Pallas kernels for 21%

profile of v1, /device:TPU:0, one launch (start us, length us, event | category | flops | bytes accessed | tf_op | source)
XLA Modules:
  0.0 238.4 jit_solution(18376411379808402664)
XLA Ops:
  1.3 3.9 %fusion = f32[512]{0:T(512)S(1)} fusion(bf16[512,5376]{1,0:T(8,128)(2,1)} %param.11), kind=kLoop, calls=%fused_computation.2 | loop fusion | flops 8257024 | bytes 5507072 | tf_op jit(solution)/shard_map/reduce_sum | solution.py:286
  7.5 3.0 %convolution_convert_fusion.2 = bf16[512,512]{1,0:T(8,128)(2,1)S(1)} fusion(bf16[512,5376]{1,0:T(8,128)(2,1)S(1)} %fusion.2, bf16[5376,512]{1,0:T(8,128)(2,1)S(1)} %bitcast.39), kind=kOutput, calls=%fused_computation.16 | convolution fusion | flops 2818834432 | bytes 11534336 | tf_op jit(solution)/shard_map/dot_general | solution.py:290
  10.5 3.0 %convolution_convert_fusion.1 = bf16[512,512]{1,0:T(8,128)(2,1)S(1)} fusion(bf16[512,5376]{1,0:T(8,128)(2,1)S(1)} %fusion.2, bf16[5376,512]{1,0:T(8,128)(2,1)S(1)} %bitcast.41), kind=kOutput, calls=%fused_computation.15 | convolution fusion | flops 2818834432 | bytes 11534336 | tf_op jit(solution)/shard_map/dot_general | solution.py:291
  13.7 4.9 %collective-permute-start = (bf16[512,512]{1,0:T(8,128)(2,1)S(1)}, bf16[512,512]{1,0:T(8,128)(2,1)S(1)}, u32[]{:S(2)}, u32[]{:S(2)}) collective-permute-start(bf16[512,512]{1,0:T(8,128)(2,1)S(1)} %pad_maximum_fusion.1.k0_ref.v0_ref), channel_id=1, source_target_pairs={{0,8},{4,12},{8,16},{12,20},{16,24},{20,28},{1,9},{5,13},{9,17},{1... | collective-permute-start | bytes 1572872 | tf_op jit(solution)/shard_map/ppermute | solution.py:26
  18.7 6.8 %convolution_convert_fusion.q_ref = bf16[512,1024]{1,0:T(8,128)(2,1)} fusion(bf16[512,5376]{1,0:T(8,128)(2,1)S(1)} %fusion.2, bf16[5376,1024]{1,0:T(8,128)(2,1)S(1)} %bitcast.37), kind=kOutput, calls=%fused_computation.12 | convolution fusion | flops 5637668864 | bytes 17563648 | tf_op jit(solution)/shard_map/dot_general | solution.py:300
  25.5 4.2 %collective-permute-done.k2_ref.v2_ref = bf16[512,512]{1,0:T(8,128)(2,1)S(1)} collective-permute-done((bf16[512,512]{1,0:T(8,128)(2,1)S(1)}, bf16[512,512]{1,0:T(8,128)(2,1)S(1)}, u32[]{:S(2)}, u32[]{:S(2)}) %collective-permute-start) | collective-permute-done | bytes 524320 | tf_op jit(solution)/shard_map/ppermute | solution.py:26
  30.7 8.3 %copy.25 = bf16[512,5376]{0,1:T(8,128)(2,1)} copy(bf16[512,5376]{1,0:T(8,128)(2,1)} %param.19) | data formatting | bytes 11010048 | tf_op jit(solution)/shard_map/optimization_barrier | solution.py:52
  39.0 3.5 %dynamic-slice_bitcast_fusion = bf16[4,672,512]{2,1,0:T(8,128)(2,1)} fusion(bf16[4,2,672,512]{3,2,1,0:T(8,128)(2,1)} %bitcast.31, s32[]{:T(128)S(6)} %select_n.94), kind=kLoop, calls=%fused_computation.11 | loop fusion | bytes 5505028 | tf_op jit(solution)/shard_map/jit(dynamic_index_in_dim)/squeeze | solution.py:317
  42.5 4.4 %collective-permute-start.5 = (bf16[512,512]{1,0:T(8,128)(2,1)S(1)}, bf16[512,512]{1,0:T(8,128)(2,1)S(1)}, u32[]{:S(2)}, u32[]{:S(2)}) collective-permute-start(bf16[512,512]{1,0:T(8,128)(2,1)S(1)} %pad_maximum_fusion.2.k0_ref.v0_ref), channel_id=1, source_target_pairs={{0,8},{4,12},{8,16},{12,20},{16,24},{20,28},{1,9},{5,13},{9,17},{1... | collective-permute-start | bytes 1572872 | tf_op jit(solution)/shard_map/ppermute | solution.py:26
  50.6 2.7 %collective-permute-start.11 = (bf16[128,1408]{1,0:T(8,128)(2,1)S(1)}, bf16[128,1408]{1,0:T(8,128)(2,1)S(1)}, u32[]{:S(2)}, u32[]{:S(2)}) collective-permute-start(bf16[128,1408]{1,0:T(8,128)(2,1)S(1)} %pad.20), channel_id=1, source_target_pairs={{0,2},{1,3},{2,0},{3,1},{4,6},{5,7},{6,4},{7,5},{8,10},{9,11},{10,... | collective-permute-start | bytes 1081352 | tf_op jit(solution)/shard_map/ppermute | solution.py:31
  54.9 3.8 %collective-permute-done.5.k2_ref.v2_ref = bf16[512,512]{1,0:T(8,128)(2,1)S(1)} collective-permute-done((bf16[512,512]{1,0:T(8,128)(2,1)S(1)}, bf16[512,512]{1,0:T(8,128)(2,1)S(1)}, u32[]{:S(2)}, u32[]{:S(2)}) %collective-permute-start.5) | collective-permute-done | bytes 524320 | tf_op jit(solution)/shard_map/ppermute | solution.py:26
  58.9 3.3 %collective-permute-done.10 = bf16[128,1408]{1,0:T(8,128)(2,1)S(1)} collective-permute-done((bf16[128,1408]{1,0:T(8,128)(2,1)S(1)}, bf16[128,1408]{1,0:T(8,128)(2,1)S(1)}, u32[]{:S(2)}, u32[]{:S(2)}) %collective-permute-start.10) | collective-permute-done | bytes 360480 | tf_op jit(solution)/shard_map/ppermute | solution.py:31
  62.2 14.8 %collective-permute-done.11 = bf16[128,1408]{1,0:T(8,128)(2,1)S(1)} collective-permute-done((bf16[128,1408]{1,0:T(8,128)(2,1)S(1)}, bf16[128,1408]{1,0:T(8,128)(2,1)S(1)}, u32[]{:S(2)}, u32[]{:S(2)}) %collective-permute-start.11) | collective-permute-done | bytes 360480 | tf_op jit(solution)/shard_map/ppermute | solution.py:31
  77.9 7.0 %attention.3 = (bf16[512,512]{1,0:T(8,128)(2,1)}, bf16[512,512]{1,0:T(8,128)(2,1)}) custom-call(s32[1]{0:T(128)} %bitcast.pos_ref, bf16[512,1024]{1,0:T(8,128)(2,1)} %convolution_convert_fusion.q_ref, bf16[512,512]{1,0:T(8,128)(2,1)} %copy-done.9, bf16[512,512]{1,0:T(8,128)(2,1)} %copy-done.14, bf16[512,512]{1,0:T(8,128)(2,1)} %copy-done.8, ...), custom_call_target="tpu_custom_call" | custom-call | flops 2684354560 | bytes 2621440 | tf_op jit(solution)/shard_map/attention/pallas_call | solution.py:124
  88.6 7.9 %grad_terms.3 = (bf16[2,672,512]{2,1,0:T(8,128)(2,1)}, bf16[2,672,512]{2,1,0:T(8,128)(2,1)}) custom-call(s32[8]{0:T(128)} %pad_add_fusion.1.tab_ref, bf16[8,672,512]{2,1,0:T(8,128)(2,1)} %bitcast.32, bf16[4,672,512]{2,1,0:T(8,128)(2,1)} %collective-permute-done.20.cot1_ref, bf16[512,512]{1,0:T(8,128)(2,1)} %get-tuple-element.24.att0_ref, ...), custom_call_target="tpu_custom_call" | custom-call | flops 2818572288 | bytes 8257536 | tf_op jit(solution)/shard_map/grad_terms/pallas_call | solution.py:166
  98.5 7.1 %attention.2 = (bf16[512,512]{1,0:T(8,128)(2,1)}, bf16[512,512]{1,0:T(8,128)(2,1)}) custom-call(s32[1]{0:T(128)} %bitcast.pos_ref, bf16[512,1024]{1,0:T(8,128)(2,1)} %convolution_convert_fusion.q_ref, bf16[512,512]{1,0:T(8,128)(2,1)} %copy-done.7, bf16[512,512]{1,0:T(8,128)(2,1)} %collective-permute-done.1.k1_ref.v1_ref, bf16[512,512]{1,0:T(8,128)(2,1)} %copy-done.6, ...), custom_call_target="tpu_custom_call" | custom-call | flops 2684354560 | bytes 2621440 | tf_op jit(solution)/shard_map/attention/pallas_call | solution.py:124
  105.5 6.4 %collective-permute-done.13.refs_8_.refs_4_ = bf16[384,1408]{1,0:T(8,128)(2,1)S(1)} collective-permute-done((bf16[384,1408]{1,0:T(8,128)(2,1)S(1)}, bf16[384,1408]{1,0:T(8,128)(2,1)S(1)}, u32[]{:S(2)}, u32[]{:S(2)}) %collective-permute-start.13) | collective-permute-done | bytes 1081376 | tf_op jit(solution)/shard_map/ppermute | solution.py:36
  114.3 8.2 %collective-permute-start.2 = (bf16[512,512]{1,0:T(8,128)(2,1)}, bf16[512,512]{1,0:T(8,128)(2,1)}, u32[]{:S(2)}, u32[]{:S(2)}) collective-permute-start(bf16[512,512]{1,0:T(8,128)(2,1)} %get-tuple-element.21.refs_0_), channel_id=1, source_target_pairs={{0,1},{1,2},{2,3},{3,0},{4,5},{5,6},{6,7},{7,4},{8,9},{9,10},{10,1... | collective-permute-start | bytes 1572872 | tf_op jit(solution)/shard_map/ppermute | solution.py:31
  123.0 7.9 %grad_terms.2 = (bf16[2,672,512]{2,1,0:T(8,128)(2,1)}, bf16[2,672,512]{2,1,0:T(8,128)(2,1)}) custom-call(s32[8]{0:T(128)} %pad_add_fusion.tab_ref, bf16[8,672,512]{2,1,0:T(8,128)(2,1)} %bitcast.33, bf16[4,672,512]{2,1,0:T(8,128)(2,1)} %collective-permute-done.20.cot1_ref, bf16[512,512]{1,0:T(8,128)(2,1)} %get-tuple-element.30.att0_ref, ...), custom_call_target="tpu_custom_call" | custom-call | flops 2818572288 | bytes 8257536 | tf_op jit(solution)/shard_map/grad_terms/pallas_call | solution.py:166
  131.1 5.5 %collective-permute-done.2.refs_2_ = bf16[512,512]{1,0:T(8,128)(2,1)} collective-permute-done((bf16[512,512]{1,0:T(8,128)(2,1)}, bf16[512,512]{1,0:T(8,128)(2,1)}, u32[]{:S(2)}, u32[]{:S(2)}) %collective-permute-start.2) | collective-permute-done | bytes 524320 | tf_op jit(solution)/shard_map/ppermute | solution.py:31
  137.6 10.2 %collective-permute-done.7.refs_3_ = bf16[512,512]{1,0:T(8,128)(2,1)} collective-permute-done((bf16[512,512]{1,0:T(8,128)(2,1)}, bf16[512,512]{1,0:T(8,128)(2,1)}, u32[]{:S(2)}, u32[]{:S(2)}) %collective-permute-start.7) | collective-permute-done | bytes 524320 | tf_op jit(solution)/shard_map/ppermute | solution.py:31
  147.9 9.1 %collective-permute-done.3.refs_4_ = bf16[512,512]{1,0:T(8,128)(2,1)} collective-permute-done((bf16[512,512]{1,0:T(8,128)(2,1)}, bf16[512,512]{1,0:T(8,128)(2,1)}, u32[]{:S(2)}, u32[]{:S(2)}) %collective-permute-start.3) | collective-permute-done | bytes 524320 | tf_op jit(solution)/shard_map/ppermute | solution.py:31
  156.9 9.2 %collective-permute-done.15.refs_10_.refs_6_ = bf16[384,1408]{1,0:T(8,128)(2,1)} collective-permute-done((bf16[384,1408]{1,0:T(8,128)(2,1)S(1)}, bf16[384,1408]{1,0:T(8,128)(2,1)}, u32[]{:S(2)}, u32[]{:S(2)}) %collective-permute-start.15) | collective-permute-done | bytes 1081376 | tf_op jit(solution)/shard_map/ppermute | solution.py:36
  166.2 8.2 %collective-permute-start.8 = (bf16[512,512]{1,0:T(8,128)(2,1)}, bf16[512,512]{1,0:T(8,128)(2,1)}, u32[]{:S(2)}, u32[]{:S(2)}) collective-permute-start(bf16[512,512]{1,0:T(8,128)(2,1)} %collective-permute-done.7.refs_3_), channel_id=1, source_target_pairs={{0,1},{1,2},{2,3},{3,0},{4,5},{5,6},{6,7},{7,4},{8,9},{9,10},{10,1... | collective-permute-start | bytes 1572872 | tf_op jit(solution)/shard_map/ppermute | solution.py:31
  174.4 3.3 %constant_dynamic-slice_fusion.1 = bf16[1024,1344]{1,0:T(8,128)(2,1)S(1)} fusion(bf16[1024,5376]{1,0:T(8,128)(2,1)} %param.16, s32[]{:T(128)S(6)} %select_n.81), kind=kLoop, calls=%fused_computation.37 | loop fusion | bytes 5505028 | tf_op jit(solution)/shard_map/dynamic_slice | solution.py:336
  183.0 3.0 %turned.1 = bf16[768,1024]{1,0:T(8,128)(2,1)} custom-call(bf16[1024,768]{1,0:T(8,128)(2,1)} %pad.22.x_ref), custom_call_target="tpu_custom_call" | custom-call | tf_op jit(solution)/shard_map/turned/pallas_call | solution.py:258
  194.4 10.9 %project.2.refs_2_ = f32[512,1408]{1,0:T(8,128)} custom-call(s32[1]{0:T(128)} %bitcast.pos_ref, bf16[512,512]{1,0:T(8,128)(2,1)} %get-tuple-element.21.refs_0_, bf16[512,512]{1,0:T(8,128)(2,1)} %get-tuple-element.23.refs_1_, bf16[512,512]{1,0:T(8,128)(2,1)} %collective-permute-done.2.refs_2_, bf16[512,512]{1,0:T(8,128)(2,1)} %collective-permute-done.7.refs_3_, ...), custom_call_target="tpu_custom_call" | custom-call | flops 4429185024 | bytes 17563648 | tf_op jit(solution)/shard_map/project/pallas_call | solution.py:234
  205.3 10.8 %collective-permute-done.9.refs_1_ = bf16[512,512]{1,0:T(8,128)(2,1)} collective-permute-done((bf16[512,512]{1,0:T(8,128)(2,1)}, bf16[512,512]{1,0:T(8,128)(2,1)}, u32[]{:S(2)}, u32[]{:S(2)}) %collective-permute-start.9) | collective-permute-done | bytes 524320 | tf_op jit(solution)/shard_map/ppermute | solution.py:31
  216.1 6.9 %project.3 = bf16[512,1344]{1,0:T(8,128)(2,1)} custom-call(s32[1]{0:T(128)} %bitcast.pos_ref, bf16[512,512]{1,0:T(8,128)(2,1)} %collective-permute-done.4.refs_0_, bf16[512,512]{1,0:T(8,128)(2,1)} %collective-permute-done.9.refs_1_, f32[512,1408]{1,0:T(8,128)} %project.2.refs_2_, bf16[384,1408]{1,0:T(8,128)(2,1)} %copy-done.1, bf16[384,1408]{1,0:T(8,128)(2,1)} %copy-done.3, ...), custom_call_target="tpu_custom_call" | custom-call | flops 1476395008 | bytes 9699328 | tf_op jit(solution)/shard_map/project/pallas_call | solution.py:234
  222.9 2.5 %copy.26 = bf16[512,1344]{0,1:T(8,128)(2,1)} copy(bf16[512,1344]{1,0:T(8,128)(2,1)} %project.3) | data formatting | bytes 2752512
  231.1 3.2 %collective-permute-done.28 = f32[8]{0:T(128)S(1)} collective-permute-done((f32[8]{0:T(128)S(1)}, f32[8]{0:T(128)S(1)}, u32[]{:S(2)}, u32[]{:S(2)}) %collective-permute-start.28) | collective-permute-done | bytes 64 | tf_op jit(solution)/shard_map/ppermute | solution.py:36
  234.6 3.3 %collective-permute-done.29 = f32[8]{0:T(128)S(1)} collective-permute-done((f32[8]{0:T(128)S(1)}, f32[8]{0:T(128)S(1)}, u32[]{:S(2)}, u32[]{:S(2)}) %collective-permute-start.29) | collective-permute-done | bytes 64 | tf_op jit(solution)/shard_map/ppermute | solution.py:36
  (126 shorter events, 40.3 us)
Async XLA Ops:
  13.7 16.0 %collective-permute-start = (bf16[512,512]{1,0:T(8,128)(2,1)S(1)}, bf16[512,512]{1,0:T(8,128)(2,1)S(1)}, u32[]{:S(2)}, u32[]{:S(2)}) collective-permute-start(bf16[512,512]{1,0:T(8,128)(2,1)S(1)} %pad_maximum_fusion.1.k0_ref.v0_ref), channel_id=1, source_target_pairs={{0,8},{4,12},{8,16},{12,20},{16,24},{20,28},{1,9},{5,13},{9,17},{1... | collective-permute-start | bytes 1572872 | tf_op jit(solution)/shard_map/ppermute | solution.py:26
  42.5 46.1 %collective-permute-start.20 = (bf16[4,672,512]{2,1,0:T(8,128)(2,1)}, bf16[4,672,512]{2,1,0:T(8,128)(2,1)}, u32[]{:S(2)}, u32[]{:S(2)}) collective-permute-start(bf16[4,672,512]{2,1,0:T(8,128)(2,1)} %dynamic-slice_bitcast_fusion), channel_id=1, source_target_pairs={{0,4},{4,0},{8,12},{12,8},{16,20},{20,16},{24,28},{28,24},{1,5},{5... | collective-permute-start | bytes 8257544 | tf_op jit(solution)/shard_map/ppermute | solution.py:36
  42.5 16.2 %collective-permute-start.5 = (bf16[512,512]{1,0:T(8,128)(2,1)S(1)}, bf16[512,512]{1,0:T(8,128)(2,1)S(1)}, u32[]{:S(2)}, u32[]{:S(2)}) collective-permute-start(bf16[512,512]{1,0:T(8,128)(2,1)S(1)} %pad_maximum_fusion.2.k0_ref.v0_ref), channel_id=1, source_target_pairs={{0,8},{4,12},{8,16},{12,20},{16,24},{20,28},{1,9},{5,13},{9,17},{1... | collective-permute-start | bytes 1572872 | tf_op jit(solution)/shard_map/ppermute | solution.py:26
  48.9 13.3 %collective-permute-start.10 = (bf16[128,1408]{1,0:T(8,128)(2,1)S(1)}, bf16[128,1408]{1,0:T(8,128)(2,1)S(1)}, u32[]{:S(2)}, u32[]{:S(2)}) collective-permute-start(bf16[128,1408]{1,0:T(8,128)(2,1)S(1)} %pad.19), channel_id=1, source_target_pairs={{0,1},{1,2},{2,3},{3,0},{4,5},{5,6},{6,7},{7,4},{8,9},{9,10},{10,1... | collective-permute-start | bytes 1081352 | tf_op jit(solution)/shard_map/ppermute | solution.py:31
  50.6 26.4 %collective-permute-start.11 = (bf16[128,1408]{1,0:T(8,128)(2,1)S(1)}, bf16[128,1408]{1,0:T(8,128)(2,1)S(1)}, u32[]{:S(2)}, u32[]{:S(2)}) collective-permute-start(bf16[128,1408]{1,0:T(8,128)(2,1)S(1)} %pad.20), channel_id=1, source_target_pairs={{0,2},{1,3},{2,0},{3,1},{4,6},{5,7},{6,4},{7,5},{8,10},{9,11},{10,... | collective-permute-start | bytes 1081352 | tf_op jit(solution)/shard_map/ppermute | solution.py:31
  53.3 23.7 %collective-permute-start.12 = (bf16[128,1408]{1,0:T(8,128)(2,1)S(1)}, bf16[128,1408]{1,0:T(8,128)(2,1)S(1)}, u32[]{:S(2)}, u32[]{:S(2)}) collective-permute-start(bf16[128,1408]{1,0:T(8,128)(2,1)S(1)} %pad.21), channel_id=1, source_target_pairs={{0,3},{1,0},{2,1},{3,2},{4,7},{5,4},{6,5},{7,6},{8,11},{9,8},{10,9... | collective-permute-start | bytes 1081352 | tf_op jit(solution)/shard_map/ppermute | solution.py:31
  58.8 18.2 %collective-permute-start.6 = (bf16[512,512]{1,0:T(8,128)(2,1)S(1)}, bf16[512,512]{1,0:T(8,128)(2,1)S(1)}, u32[]{:S(2)}, u32[]{:S(2)}) collective-permute-start(bf16[512,512]{1,0:T(8,128)(2,1)S(1)} %broadcast_select_fusion), channel_id=1, source_target_pairs={{0,4},{4,0},{8,12},{12,8},{16,20},{20,16},{24,28},{28,24},{1,5},{5... | collective-permute-start | bytes 1572872 | tf_op jit(solution)/shard_map/ppermute | solution.py:36
  84.9 3.3 %collective-permute-start.24 = (bf16[512,512]{1,0:T(8,128)(2,1)}, bf16[512,512]{1,0:T(8,128)(2,1)}, u32[]{:S(2)}, u32[]{:S(2)}) collective-permute-start(bf16[512,512]{1,0:T(8,128)(2,1)} %get-tuple-element.24.att0_ref), channel_id=1, source_target_pairs={{0,4},{4,0},{8,12},{12,8},{16,20},{20,16},{24,28},{28,24},{1,5},{5... | collective-permute-start | bytes 1572872 | tf_op jit(solution)/shard_map/ppermute | solution.py:36
  85.0 26.9 %collective-permute-start.13 = (bf16[384,1408]{1,0:T(8,128)(2,1)S(1)}, bf16[384,1408]{1,0:T(8,128)(2,1)S(1)}, u32[]{:S(2)}, u32[]{:S(2)}) collective-permute-start(bf16[384,1408]{1,0:T(8,128)(2,1)S(1)} %constant_dynamic-update-slice_fusion.refs_7_.refs_3_), channel_id=1, source_target_pairs={{0,8},{4,12},{8,0},{12,4},{16,24},{20,28},{24,16},{28,20},{1,9},{5... | collective-permute-start | bytes 3244040 | tf_op jit(solution)/shard_map/ppermute | solution.py:36
  87.4 26.8 %collective-permute-start.14 = (bf16[384,1408]{1,0:T(8,128)(2,1)S(1)}, bf16[384,1408]{1,0:T(8,128)(2,1)}, u32[]{:S(2)}, u32[]{:S(2)}) collective-permute-start(bf16[384,1408]{1,0:T(8,128)(2,1)S(1)} %constant_dynamic-update-slice_fusion.refs_7_.refs_3_), channel_id=1, source_target_pairs={{0,16},{4,20},{8,24},{12,28},{16,0},{20,4},{24,8},{28,12},{1,17},{... | collective-permute-start | bytes 3244040 | tf_op jit(solution)/shard_map/ppermute | solution.py:36
  87.4 11.0 %collective-permute-start.1 = (bf16[512,512]{1,0:T(8,128)(2,1)}, bf16[512,512]{1,0:T(8,128)(2,1)}, u32[]{:S(2)}, u32[]{:S(2)}) collective-permute-start(bf16[512,512]{1,0:T(8,128)(2,1)} %broadcast_select_fusion.1), channel_id=1, source_target_pairs={{0,4},{4,0},{8,12},{12,8},{16,20},{20,16},{24,28},{28,24},{1,5},{5... | collective-permute-start | bytes 1572872 | tf_op jit(solution)/shard_map/ppermute | solution.py:36
  88.3 42.7 %collective-permute-start.16 = (bf16[384,1408]{1,0:T(8,128)(2,1)S(1)}, bf16[384,1408]{1,0:T(8,128)(2,1)S(1)}, u32[]{:S(2)}, u32[]{:S(2)}) collective-permute-start(bf16[384,1408]{1,0:T(8,128)(2,1)S(1)} %constant_dynamic-update-slice_fusion.refs_7_.refs_3_), channel_id=1, source_target_pairs={{0,4},{4,0},{8,12},{12,8},{16,20},{20,16},{24,28},{28,24},{1,5},{5... | collective-permute-start | bytes 3244040 | tf_op jit(solution)/shard_map/ppermute | solution.py:36
  96.4 77.9 %collective-permute-start.25 = (bf16[2,672,512]{2,1,0:T(8,128)(2,1)}, bf16[2,672,512]{2,1,0:T(8,128)(2,1)}, u32[]{:S(2)}, u32[]{:S(2)}) collective-permute-start(bf16[2,672,512]{2,1,0:T(8,128)(2,1)} %get-tuple-element.34), channel_id=1, source_target_pairs={{0,16},{4,20},{8,24},{12,28},{16,0},{20,4},{24,8},{28,12},{1,17},{... | collective-permute-start | bytes 4128776 | tf_op jit(solution)/shard_map/ppermute | solution.py:36
  105.5 17.5 %collective-permute-start.21 = (bf16[512,512]{1,0:T(8,128)(2,1)}, bf16[512,512]{1,0:T(8,128)(2,1)}, u32[]{:S(2)}, u32[]{:S(2)}) collective-permute-start(bf16[512,512]{1,0:T(8,128)(2,1)} %get-tuple-element.30.att0_ref), channel_id=1, source_target_pairs={{0,4},{4,0},{8,12},{12,8},{16,20},{20,16},{24,28},{28,24},{1,5},{5... | collective-permute-start | bytes 1572872 | tf_op jit(solution)/shard_map/ppermute | solution.py:36
  111.9 35.9 %copy-start.3 = (bf16[384,1408]{1,0:T(8,128)(2,1)}, bf16[384,1408]{1,0:T(8,128)(2,1)S(1)}, u32[]{:S(2)}) copy-start(bf16[384,1408]{1,0:T(8,128)(2,1)S(1)} %collective-permute-done.13.refs_8_.refs_4_) | copy-start | bytes 3244036
  111.9 54.2 %collective-permute-start.15 = (bf16[384,1408]{1,0:T(8,128)(2,1)S(1)}, bf16[384,1408]{1,0:T(8,128)(2,1)}, u32[]{:S(2)}, u32[]{:S(2)}) collective-permute-start(bf16[384,1408]{1,0:T(8,128)(2,1)S(1)} %collective-permute-done.13.refs_8_.refs_4_), channel_id=1, source_target_pairs={{0,16},{4,20},{8,24},{12,28},{16,0},{20,4},{24,8},{28,12},{1,17},{... | collective-permute-start | bytes 3244040 | tf_op jit(solution)/shard_map/ppermute | solution.py:36
  114.3 22.3 %collective-permute-start.2 = (bf16[512,512]{1,0:T(8,128)(2,1)}, bf16[512,512]{1,0:T(8,128)(2,1)}, u32[]{:S(2)}, u32[]{:S(2)}) collective-permute-start(bf16[512,512]{1,0:T(8,128)(2,1)} %get-tuple-element.21.refs_0_), channel_id=1, source_target_pairs={{0,1},{1,2},{2,3},{3,0},{4,5},{5,6},{6,7},{7,4},{8,9},{9,10},{10,1... | collective-permute-start | bytes 1572872 | tf_op jit(solution)/shard_map/ppermute | solution.py:31
  123.0 24.8 %collective-permute-start.7 = (bf16[512,512]{1,0:T(8,128)(2,1)}, bf16[512,512]{1,0:T(8,128)(2,1)}, u32[]{:S(2)}, u32[]{:S(2)}) collective-permute-start(bf16[512,512]{1,0:T(8,128)(2,1)} %get-tuple-element.23.refs_1_), channel_id=1, source_target_pairs={{0,1},{1,2},{2,3},{3,0},{4,5},{5,6},{6,7},{7,4},{8,9},{9,10},{10,1... | collective-permute-start | bytes 1572872 | tf_op jit(solution)/shard_map/ppermute | solution.py:31
  130.9 46.7 %copy-start.4 = (bf16[384,1408]{1,0:T(8,128)(2,1)}, bf16[384,1408]{1,0:T(8,128)(2,1)S(1)}, u32[]{:S(2)}) copy-start(bf16[384,1408]{1,0:T(8,128)(2,1)S(1)} %collective-permute-done.16.refs_11_.refs_7_) | copy-start | bytes 3244036
  130.9 59.6 %collective-permute-start.22 = (bf16[2,672,512]{2,1,0:T(8,128)(2,1)}, bf16[2,672,512]{2,1,0:T(8,128)(2,1)}, u32[]{:S(2)}, u32[]{:S(2)}) collective-permute-start(bf16[2,672,512]{2,1,0:T(8,128)(2,1)} %get-tuple-element.32), channel_id=1, source_target_pairs={{0,8},{4,12},{8,0},{12,4},{16,24},{20,28},{24,16},{28,20},{1,9},{5... | collective-permute-start | bytes 4128776 | tf_op jit(solution)/shard_map/ppermute | solution.py:36
  136.6 20.4 %collective-permute-start.3 = (bf16[512,512]{1,0:T(8,128)(2,1)}, bf16[512,512]{1,0:T(8,128)(2,1)}, u32[]{:S(2)}, u32[]{:S(2)}) collective-permute-start(bf16[512,512]{1,0:T(8,128)(2,1)} %collective-permute-done.2.refs_2_), channel_id=1, source_target_pairs={{0,1},{1,2},{2,3},{3,0},{4,5},{5,6},{6,7},{7,4},{8,9},{9,10},{10,1... | collective-permute-start | bytes 1572872 | tf_op jit(solution)/shard_map/ppermute | solution.py:31
  147.8 40.6 %collective-permute-start.17 = (bf16[384,1408]{1,0:T(8,128)(2,1)S(1)}, bf16[384,1408]{1,0:T(8,128)(2,1)}, u32[]{:S(2)}, u32[]{:S(2)}) collective-permute-start(bf16[384,1408]{1,0:T(8,128)(2,1)S(1)} %collective-permute-done.13.refs_8_.refs_4_), channel_id=1, source_target_pairs={{0,4},{4,0},{8,12},{12,8},{16,20},{20,16},{24,28},{28,24},{1,5},{5... | collective-permute-start | bytes 3244040 | tf_op jit(solution)/shard_map/ppermute | solution.py:36
  156.9 36.6 %collective-permute-start.18 = (bf16[384,1408]{1,0:T(8,128)(2,1)}, bf16[384,1408]{1,0:T(8,128)(2,1)}, u32[]{:S(2)}, u32[]{:S(2)}) collective-permute-start(bf16[384,1408]{1,0:T(8,128)(2,1)} %collective-permute-done.14.refs_9_.refs_5_), channel_id=1, source_target_pairs={{0,4},{4,0},{8,12},{12,8},{16,20},{20,16},{24,28},{28,24},{1,5},{5... | collective-permute-start | bytes 3244040 | tf_op jit(solution)/shard_map/ppermute | solution.py:36
  166.2 22.2 %collective-permute-start.8 = (bf16[512,512]{1,0:T(8,128)(2,1)}, bf16[512,512]{1,0:T(8,128)(2,1)}, u32[]{:S(2)}, u32[]{:S(2)}) collective-permute-start(bf16[512,512]{1,0:T(8,128)(2,1)} %collective-permute-done.7.refs_3_), channel_id=1, source_target_pairs={{0,1},{1,2},{2,3},{3,0},{4,5},{5,6},{6,7},{7,4},{8,9},{9,10},{10,1... | collective-permute-start | bytes 1572872 | tf_op jit(solution)/shard_map/ppermute | solution.py:31
  174.4 20.0 %collective-permute-start.19 = (bf16[384,1408]{1,0:T(8,128)(2,1)}, bf16[384,1408]{1,0:T(8,128)(2,1)}, u32[]{:S(2)}, u32[]{:S(2)}) collective-permute-start(bf16[384,1408]{1,0:T(8,128)(2,1)} %collective-permute-done.15.refs_10_.refs_6_), channel_id=1, source_target_pairs={{0,4},{4,0},{8,12},{12,8},{16,20},{20,16},{24,28},{28,24},{1,5},{5... | collective-permute-start | bytes 3244040 | tf_op jit(solution)/shard_map/ppermute | solution.py:36
  188.3 17.0 %collective-permute-start.4 = (bf16[512,512]{1,0:T(8,128)(2,1)}, bf16[512,512]{1,0:T(8,128)(2,1)}, u32[]{:S(2)}, u32[]{:S(2)}) collective-permute-start(bf16[512,512]{1,0:T(8,128)(2,1)} %collective-permute-done.3.refs_4_), channel_id=1, source_target_pairs={{0,1},{1,2},{2,3},{3,0},{4,5},{5,6},{6,7},{7,4},{8,9},{9,10},{10,1... | collective-permute-start | bytes 1572872 | tf_op jit(solution)/shard_map/ppermute | solution.py:31
  188.4 27.7 %collective-permute-start.9 = (bf16[512,512]{1,0:T(8,128)(2,1)}, bf16[512,512]{1,0:T(8,128)(2,1)}, u32[]{:S(2)}, u32[]{:S(2)}) collective-permute-start(bf16[512,512]{1,0:T(8,128)(2,1)} %collective-permute-done.8.refs_5_), channel_id=1, source_target_pairs={{0,1},{1,2},{2,3},{3,0},{4,5},{5,6},{6,7},{7,4},{8,9},{9,10},{10,1... | collective-permute-start | bytes 1572872 | tf_op jit(solution)/shard_map/ppermute | solution.py:31
  190.5 34.9 %collective-permute-start.26 = (bf16[1,672,512]{2,1,0:T(8,128)(2,1)S(1)}, bf16[1,672,512]{2,1,0:T(8,128)(2,1)}, u32[]{:S(2)}, u32[]{:S(2)}) collective-permute-start(bf16[1,672,512]{2,1,0:T(8,128)(2,1)S(1)} %slice.43), channel_id=1, source_target_pairs={{0,8},{4,12},{8,0},{12,4},{16,24},{20,28},{24,16},{28,20},{1,9},{5... | collective-permute-start | bytes 2064392 | tf_op jit(solution)/shard_map/ppermute | solution.py:36
  193.6 33.3 %collective-permute-start.23 = (bf16[1,672,512]{2,1,0:T(8,128)(2,1)}, bf16[1,672,512]{2,1,0:T(8,128)(2,1)}, u32[]{:S(2)}, u32[]{:S(2)}) collective-permute-start(bf16[1,672,512]{2,1,0:T(8,128)(2,1)} %slice.41), channel_id=1, source_target_pairs={{0,16},{4,20},{8,24},{12,28},{16,0},{20,4},{24,8},{28,12},{1,17},{... | collective-permute-start | bytes 2064392 | tf_op jit(solution)/shard_map/ppermute | solution.py:36
  228.8 1.9 collective-permute-start.27
  230.8 3.6 %collective-permute-start.28 = (f32[8]{0:T(128)S(1)}, f32[8]{0:T(128)S(1)}, u32[]{:S(2)}, u32[]{:S(2)}) collective-permute-start(f32[8]{0:T(128)S(1)} %add.136), channel_id=1, source_target_pairs={{0,8},{4,12},{8,0},{12,4},{16,24},{20,28},{24,16},{28,20},{1,9},{5... | collective-permute-start | bytes 104 | tf_op jit(solution)/shard_map/ppermute | solution.py:36
  234.3 3.6 %collective-permute-start.29 = (f32[8]{0:T(128)S(1)}, f32[8]{0:T(128)S(1)}, u32[]{:S(2)}, u32[]{:S(2)}) collective-permute-start(f32[8]{0:T(128)S(1)} %add.137), channel_id=1, source_target_pairs={{0,16},{4,20},{8,24},{12,28},{16,0},{20,4},{24,8},{28,12},{1,17},{... | collective-permute-start | bytes 104 | tf_op jit(solution)/shard_map/ppermute | solution.py:36
  (20 other events, 177.9 us)

commit v2 on v1

--- a/solution.py
+++ b/solution.py
@@ -34,6 +34,16 @@
 def swap(value, axis, bit):
     count = lax.axis_size(axis)
     return lax.ppermute(value, axis, [(i, i ^ bit) for i in range(count)])
+
+
+def window_of(cols):
+    step = math.gcd(cols, 128)
+    return -(-(cols + 128 - step) // 128) * 128
+
+
+def window_start(width, cols, index):
+    first = index * cols // 128 * 128
+    return jnp.minimum(first, width - window_of(cols))
 
 
 def hard_concrete(mask_logit, noise_draw):
@@ -139,47 +149,106 @@
     )(position, queries, kv2, kv1, kv0, kv2, kv1, kv0, gate_row)
 
 
-def terms_kernel(tab_ref, cot0_ref, cot1_ref, att0_ref, att1_ref, sent_ref, kept_ref, *, sent):
+def lead_kernel(tab_ref, cot_ref, away_ref, home_ref, held, *, steps, wide):
+    index = pl.program_id(0)
+    start = pl.multiple_of(tab_ref[index], 128)
+    shift_rows = pl.multiple_of(tab_ref[steps + index], 16)
+    held[...] = cot_ref[:, pl.ds(start, wide)].T
+    block = held[pl.ds(shift_rows, away_ref.shape[1])]
+
+    @pl.when(index < steps // 2)
+    def _():
+        away_ref[0] = block
+
+    @pl.when(index >= steps // 2)
+    def _():
+        home_ref[0] = block
+
+
+def lead_blocks(parity, cotangent, count):
+    rows, model_width = cotangent.shape
+    width = model_width // count
+    wide = window_of(width)
+    half = count // 2
+    number = jnp.arange(half, dtype=jnp.int32) * 2
+    owners = jnp.concatenate([number + 1 - parity, number + parity])
+    starts = window_start(model_width, width, owners)
+    table = jnp.concatenate([starts, owners * width - starts]).astype(jnp.int32)
+    return pl.pallas_call(
+        functools.partial(lead_kernel, steps=count, wide=wide),
+        grid_spec=pltpu.PrefetchScalarGridSpec(
+            num_scalar_prefetch=1,
+            grid=(count,),
+            in_specs=[pl.BlockSpec((rows, model_width), lambda j, tab: (0, 0))],
+            out_specs=[
+                pl.BlockSpec((1, width, rows), lambda j, tab: (jnp.minimum(j, half - 1), 0, 0)),
+                pl.BlockSpec((1, width, rows), lambda j, tab: (jnp.maximum(j - half, 0), 0, 0)),
+            ],
+            scratch_shapes=[pltpu.VMEM((wide, rows), cotangent.dtype)],
+        ),
+        out_shape=[jax.ShapeDtypeStruct((half, width, rows), cotangent.dtype)] * 2,
+        compiler_params=pltpu.CompilerParams(dimension_semantics=("arbitrary",)),
+        cost_estimate=pl.CostEstimate(
+            flops=8 * rows * model_width, bytes_accessed=4 * rows * model_width, transcendentals=0),
+        name="lead",
+    )(table, cotangent)
+
+
+def terms_kernel(tab_ref, cot0_ref, cot1_ref, att0_ref, att1_ref, *out_refs, steps):
     index = pl.program_id(0)
     total = (
         jnp.dot(cot0_ref[0], att0_ref[...], preferred_element_type=jnp.float32)
         + jnp.dot(cot1_ref[0], att1_ref[...], preferred_element_type=jnp.float32)
     ).astype(jnp.bfloat16)
-
-    @pl.when(index < sent)
-    def _():
-        sent_ref[0] = total
-
-    @pl.when(index >= sent)
-    def _():
-        kept_ref[0] = total
-
-
-def grad_terms(position, cot_blocks, cot_other, att, att_other, order):
+    sides = len(out_refs) // 2
+    part = total.shape[1] // sides
+    for side in range(sides):
+        piece = total[:, side * part:(side + 1) * part]
+        leaves = tab_ref[(1 + 3 * side) * steps + index]
+
+        @pl.when(leaves == 1)
+        def _():
+            out_refs[2 * side][0] = piece
+
+        @pl.when(leaves == 0)
+        def _():
+            out_refs[2 * side + 1][0] = piece
+
+
+def grad_terms(position, cot_blocks, cot_other, att, att_other, order, first_bits):
     _, width, rows = cot_blocks.shape
     cols = att.shape[1]
     steps = len(order)
     sent = steps // 2
     owners = position ^ jnp.array(order, jnp.int32)
-    table = jnp.concatenate([owners, owners // 2])
+    rest = []
+    for bit in first_bits:
+        leaves = [1 if r & bit else 0 for r in order]
+        rest += leaves
+        rest += [max(sum(leaves[:j + 1]) - 1, 0) for j in range(steps)]
+        rest += [max(j - sum(leaves[:j + 1]), 0) for j in range(steps)]
+    sides = len(first_bits)
+    table = jnp.concatenate([owners // 2, jnp.array(rest, jnp.int32)])
     whole = pl.BlockSpec((rows, cols), lambda j, tab: (0, 0))
+
+    def out(row):
+        return pl.BlockSpec((1, width, cols // sides), lambda j, tab: (tab[row * steps + j], 0, 0))
+
     return pl.pallas_call(
-        functools.partial(terms_kernel, sent=sent),
+        functools.partial(terms_kernel, steps=steps),
         grid_spec=pltpu.PrefetchScalarGridSpec(
             num_scalar_prefetch=1,
             grid=(steps,),
             in_specs=[
                 pl.BlockSpec((1, width, rows), lambda j, tab: (tab[j], 0, 0)),
-                pl.BlockSpec((1, width, rows), lambda j, tab: (tab[steps + j], 0, 0)),
+                pl.BlockSpec((1, width, rows), lambda j, tab: (tab[j], 0, 0)),
                 whole,
                 whole,
             ],
-            out_specs=[
-                pl.BlockSpec((1, width, cols), lambda j, tab: (jnp.minimum(j, sent - 1), 0, 0)),
-                pl.BlockSpec((1, width, cols), lambda j, tab: (jnp.maximum(j - sent, 0), 0, 0)),
-            ],
+            out_specs=[out(2 + 3 * (k // 2) + k % 2) for k in range(2 * sides)],
         ),
-        out_shape=[jax.ShapeDtypeStruct((sent, width, cols), jnp.bfloat16)] * 2,
+        out_shape=[jax.ShapeDtypeStruct((sent, width, cols // sides), jnp.bfloat16)]
+        * (2 * sides),
         compiler_params=pltpu.CompilerParams(dimension_semantics=("arbitrary",)),
         cost_estimate=pl.CostEstimate(
             flops=4 * steps * width * rows * cols,
@@ -188,7 +257,7 @@
     )(table, cot_blocks, cot_other, att, att_other)
 
 
-def project_kernel(pos_ref, *refs, turns, slots, count):
+def project_kernel(pos_ref, *refs, turns, slots, count, final):
     pairs = 2 * len(turns)
     x_refs = refs[:pairs]
     rest = list(refs[pairs:])
@@ -201,12 +270,14 @@
     for k, turn in enumerate(turns):
         group = []
         if turn == -1:
-            group.append(pltpu.make_async_copy(own_ref, weight.at[k], sems.at[k, 0]))
+            start = pl.multiple_of(pos_ref[1], 128)
+            group.append(pltpu.make_async_copy(
+                own_ref.at[:, pl.ds(start, weight.shape[2])], weight.at[k], sems.at[k, 0]))
         else:
             for index, relative in enumerate(slots):
                 start = pl.multiple_of((position ^ relative) * count, count)
                 group.append(pltpu.make_async_copy(
-                    w_refs[index].at[pl.ds(turn * count, count)], weight.at[k, pl.ds(start, count)], sems.at[k, index]))
+                    w_refs[index].at[turn], weight.at[k, pl.ds(start, count)], sems.at[k, index]))
         for copy in group:
             copy.start()
         copies.append(group)
@@ -222,17 +293,21 @@
                 preferred_element_type=jnp.float32,
             )
             total = part if total is None else total + part
-    out_ref[...] = total[:, :out_ref.shape[1]].astype(out_ref.dtype)
+    if final:
+        wide = total.shape[1]
+        total = pltpu.roll(total, lax.rem(wide - pos_ref[2], wide), 1)[:, :out_ref.shape[1]]
+    out_ref[...] = total.astype(out_ref.dtype)
 
 
 def project(position, xs, base, own, weights, slots, turns, out_cols, dtype):
     rows, middle = xs[0].shape
-    cols = weights[0].shape[1]
+    cols = weights[0].shape[2]
     whole = pl.BlockSpec(memory_space=pltpu.VMEM)
     anywhere = pl.BlockSpec(memory_space=pl.ANY)
     extra = [own] if base is None else [base]
     return pl.pallas_call(
-        functools.partial(project_kernel, turns=turns, slots=slots, count=2 * middle // len(slots)),
+        functools.partial(project_kernel, turns=turns, slots=slots, count=2 * middle // len(slots),
+                          final=base is not None),
         in_specs=[pl.BlockSpec(memory_space=pltpu.SMEM)] + [whole] * len(xs)
         + [anywhere if base is None else whole] + [anywhere] * len(weights),
         out_specs=whole,
@@ -249,16 +324,70 @@
     )(position, *xs, *extra, *weights)
 
 
-def turned_kernel(x_ref, out_ref):
-    out_ref[...] = x_ref[...].T
-
-
-def turned(x):
-    whole = pl.BlockSpec(memory_space=pltpu.VMEM)
+def finish_kernel(*refs, counts):
+    w_ref, gate_ref, grad_ref, product_ref = refs[-4:]
+    place = 0
+    for side, count in enumerate(counts):
+        total = refs[place][0].astype(jnp.float32)
+        for ref in refs[place + 1:place + count]:
+            total = total + ref[0].astype(jnp.float32)
+        place += count
+        cols = slice(side * total.shape[1], (side + 1) * total.shape[1])
+        grad_ref[:, cols] = total * gate_ref[:, cols]
+        weighted = total * w_ref[:total.shape[0], cols].astype(jnp.float32)
+        product_ref[:, cols] = jnp.sum(weighted, axis=0, keepdims=True)
+
+
+def finish(grads, w_mine, scale_row):
+    in_specs = []
+    operands = []
+    for terms in grads:
+        for array, index in terms:
+            in_specs.append(
+                pl.BlockSpec((1,) + array.shape[1:], functools.partial(first_at, index)))
+            operands.append(array)
+    width = grads[0][0][0].shape[1]
+    depth = w_mine.shape[1]
+    whole = [w_mine.shape, (1, depth)]
     return pl.pallas_call(
-        turned_kernel, in_specs=[whole], out_specs=whole,
-        out_shape=jax.ShapeDtypeStruct(x.shape[::-1], x.dtype), name="turned",
-    )(x)
+        functools.partial(finish_kernel, counts=tuple(len(terms) for terms in grads)),
+        grid=(1,),
+        in_specs=in_specs + [pl.BlockSpec(shape, lambda g: (0, 0)) for shape in whole],
+        out_specs=[pl.BlockSpec((width, depth), lambda g: (0, 0)),
+                   pl.BlockSpec((1, depth), lambda g: (0, 0))],
+        out_shape=[jax.ShapeDtypeStruct((width, depth), jnp.float32),
+                   jax.ShapeDtypeStruct((1, depth), jnp.float32)],
+        cost_estimate=pl.CostEstimate(
+            flops=8 * width * depth, bytes_accessed=12 * width * depth, transcendentals=0),
+        name="finish",
+    )(*operands, w_mine, scale_row)
+
+
+def first_at(index, step):
+    return (index, 0, 0)
+
+
+def turned_kernel(pos_ref, w_ref, out_ref, held, flipped, sem):
+    start = pl.multiple_of(pos_ref[3], 128)
+    copy = pltpu.make_async_copy(w_ref.at[:, pl.ds(start, held.shape[1])], held, sem)
+    copy.start()
+    copy.wait()
+    flipped[...] = held[...].T
+    out_ref[...] = flipped[pl.ds(pl.multiple_of(pos_ref[4], 16), out_ref.shape[0])]
+
+
+def turned(position, w_out, cols):
+    wide = window_of(cols)
+    return pl.pallas_call(
+        turned_kernel,
+        in_specs=[pl.BlockSpec(memory_space=pltpu.SMEM), pl.BlockSpec(memory_space=pl.ANY)],
+        out_specs=pl.BlockSpec(memory_space=pltpu.VMEM),
+        out_shape=jax.ShapeDtypeStruct((cols, w_out.shape[0]), w_out.dtype),
+        scratch_shapes=[pltpu.VMEM((w_out.shape[0], wide), w_out.dtype),
+                        pltpu.VMEM((wide, w_out.shape[0]), w_out.dtype),
+                        pltpu.SemaphoreType.DMA],
+        name="turned",
+    )(position, w_out)
 
 
 def body(tokens, norm_gain, w_query, w_key, value_weight, w_out, mask_logit, noise_draw, cotangent):
@@ -268,18 +397,23 @@
     n_head = lax.axis_size("head")
     p = lax.axis_index("ctx")
     z = lax.axis_index("head")
-    position = p.astype(jnp.int32).reshape(1)
     bits = [1 << k for k in range(1, n_ctx.bit_length() - 1)]
     inv_root = 1.0 / math.sqrt(tok_rows * n_ctx)
     out_cols = model_width // n_head
-    wide_cols = -(-out_cols // 128) * 128
+    own_cols = model_width // n_ctx
+    wide_cols = window_of(out_cols)
+    own_start = window_start(model_width, out_cols, z)
+    mine_start = window_start(model_width, own_cols, p)
+    scalars = jnp.stack(
+        [p, own_start, z * out_cols - own_start, mine_start, p * own_cols - mine_start]).astype(jnp.int32)
+    position = scalars[:1]
     piece = w_out.shape[0] // n_ctx
 
     mine = lax.dynamic_slice_in_dim(w_out, p * piece, piece, 0)
     turns = []
     for t in range(1, n_head):
-        block = lax.dynamic_slice_in_dim(mine, ((z + t) % n_head) * out_cols, out_cols, 1)
-        block = jnp.pad(block, ((0, 0), (0, wide_cols - out_cols)))
+        block = lax.dynamic_slice_in_dim(
+            mine, window_start(model_width, out_cols, (z + t) % n_head), wide_cols, 1)
         turns.append(rotate(block, "head", t))
 
     widened = tokens.astype(jnp.float32)
@@ -305,18 +439,13 @@
     gate_columns = jnp.repeat(gate_value, HEAD_SIZE)
     gate_row = gate_columns[None, :]
 
-    own_part = jnp.concatenate(after(tuple(turns), queries), axis=0)
+    own_part = jnp.stack(after(tuple(turns), queries))
     parts = {0: own_part}
     for bit in bits:
         for relative in list(parts):
             parts[relative | bit] = swap(parts[relative], "ctx", bit)
 
     mixed = [jnp.where(p % 2 == 0, kv_sides[h], after(kv2_sides[h], queries)) for h in range(2)]
-
-    cot_blocks = after(cotangent, mixed[0]).T.reshape(n_ctx, model_width // n_ctx, tok_rows)
-    leaving = lax.dynamic_index_in_dim(
-        cot_blocks.reshape((n_ctx // 2, 2) + cot_blocks.shape[1:]), 1 - p % 2, 1, keepdims=False)
-    cot_other = swap(leaving, "ctx", 1)
 
     attended = []
     moving = []
@@ -331,35 +460,35 @@
             chain.append(rotate(chain[-1], "head", 1))
         moving.append(chain)
         others.append(swap(att, "ctx", 1))
-
-    own_weight = jnp.pad(
-        lax.dynamic_slice_in_dim(after(w_out, attended[1]), z * out_cols, out_cols, 1),
-        ((0, 0), (0, wide_cols - out_cols)))
-
-    own_cols = model_width // n_ctx
-    w_mine = lax.dynamic_slice_in_dim(after(w_out, attended[1]), p * own_cols, own_cols, 1)
-    w_mine = turned(jnp.pad(w_mine, ((0, 0), (0, -own_cols % 128))))[:own_cols]
+        if h == 0:
+            leaving, cot_home = lead_blocks(after(p % 2, att), cotangent, n_ctx)
+            cot_other = swap(leaving, "ctx", 1)
+
+    w_mine = turned(after(scalars, attended[1]), w_out, own_cols)
 
     grads = []
+    relative = [2 * j for j in range(n_ctx // 2)]
     for h in range(2):
-        steps = bits if h == 0 else bits[::-1]
-        relative = [2 * j for j in range(n_ctx // 2)]
-        order = [r for r in relative if r & steps[0]] + [r for r in relative if not r & steps[0]]
-        sent, kept = grad_terms(
-            position, cot_blocks, cot_other, attended[h], others[h], order)
-        relative = order[len(order) // 2:]
-        for k, bit in enumerate(steps):
-            if k:
-                leave = [i for i, r in enumerate(relative) if r & bit]
-                stay = [i for i, r in enumerate(relative) if not r & bit]
-                sent = jnp.concatenate([total[i:i + 1] for i in leave], axis=0)
-                kept = jnp.concatenate([total[i:i + 1] for i in stay], axis=0)
-                relative = [relative[i] for i in stay]
-            received = swap(sent, "ctx", bit)
-            total = kept.astype(jnp.float32) + received.astype(jnp.float32)
-            if len(relative) > 1:
-                total = total.astype(jnp.bfloat16)
-        grads.append(total[0])
+        orders = (bits, bits[::-1])
+        blocks = grad_terms(
+            position, cot_home, cot_other, attended[h], others[h], relative[::-1],
+            [order[0] for order in orders])
+        for side, order in enumerate(orders):
+            sent, kept = blocks[2 * side:2 * side + 2]
+            left = [r for r in relative[::-1] if not r & order[0]]
+            held = [[(kept, i)] for i in range(len(left))]
+            for k, bit in enumerate(order):
+                if k:
+                    leave = [i for i, r in enumerate(left) if r & bit]
+                    stay = [i for i, r in enumerate(left) if not r & bit]
+                    sent = jnp.concatenate(
+                        [sum(a[i:i + 1].astype(jnp.float32) for a, i in held[index])
+                         for index in leave], axis=0).astype(jnp.bfloat16)
+                    held = [held[i] for i in stay]
+                    left = [left[i] for i in stay]
+                received = swap(sent, "ctx", bit)
+                held = [terms + [(received, i)] for i, terms in enumerate(held)]
+            grads.append(held[0])
 
     for relative in list(parts):
         parts[relative | 1] = swap(parts[relative], "ctx", 1)
@@ -370,19 +499,20 @@
     xs = [moving[h][0] for h in range(2)]
     for t in early:
         xs += [moving[h][t + 1] for h in range(2)]
-    base = project(position, xs, None, own_weight, weights, slots, (-1,) + tuple(early),
+    base = project(scalars, xs, None, w_out, weights, slots, (-1,) + tuple(early),
                    wide_cols, jnp.float32)
-    layer_out = project(position, [moving[h][-1] for h in range(2)], base, None, weights,
+    layer_out = project(scalars, [moving[h][-1] for h in range(2)], base, None, weights,
                         slots, (n_head - 2,), out_cols, jnp.bfloat16)
 
-    summed = jnp.concatenate([g.T for g in grads], axis=0)
-    grad_out_proj = summed * gate_columns[:, None] * inv_root
-
-    head_terms = jnp.sum(
-        (summed.T * w_mine.astype(jnp.float32)).reshape(-1, local_heads, HEAD_SIZE), axis=(0, 2))
-    for bit in [1] + bits:
-        head_terms = head_terms + swap(head_terms, "ctx", bit)
-    grad_logit = head_terms * inv_root * gate_slope + penalty_term
+    grad_columns, products = finish(grads, w_mine, gate_row * inv_root)
+    grad_out_proj = grad_columns.T
+    head_terms = jnp.sum(products.reshape(local_heads, HEAD_SIZE), axis=1)
+    values = [head_terms]
+    for member in range(1, n_ctx):
+        values.append(swap(head_terms, "ctx", member))
+    while len(values) > 1:
+        values = [values[i] + values[i + 1] for i in range(0, len(values), 2)]
+    grad_logit = values[0] * inv_root * gate_slope + penalty_term
     return (layer_out, grad_logit, grad_out_proj)
 
 

time: 239 us -> 231 us (0.967)
  waiting for transfers between devices: 85.4 us -> 62.7 us
  local copies, waits for them, and re-layouts: 27.2 us -> 7.68 us
  Pallas kernels: 50.6 us -> 65.6 us
  starting transfers between devices: 42.7 us -> 57.5 us
  matrix products: 12.8 us -> 15.6 us
    ppermute x9, waiting for transfers between devices: 53.7 us -> 31.9 us  [rotate(): lax.ppermute(value, axis, [(i, (i + steps) % count) for i in range(count)])]
    pallas_call x3 -> x5, Pallas kernels: 18.8 us -> 33.3 us  [the longest x2 15.9 us: grad_terms(): pl.pallas_call(functools.partial(terms_kernel, steps=steps), grid_spec=pl...]
    ppermute x19 -> x27, starting transfers between devices: 7.93 us -> 21.8 us  [swap(): return lax.ppermute(value, axis, [(i, i ^ bit) for i in range(count)])]
    optimization_barrier x1 -> x0, local copies, waits for them, and re-layouts: 8.25 us -> none  [after(): return lax.optimization_barrier((value,) + others)[0]]
    dynamic_slice x3 -> x1, local copies, waits for them, and re-layouts: 7.38 us -> 1.88 us  [body(): lax.dynamic_slice_in_dim(mine, window_start(model_width, out_cols, (z + t...]
    ppermute x2, waiting for transfers between devices: 8.08 us -> 3.19 us  [shift(): lax.ppermute(value, axis, [(i, i + steps) for i in range(count - steps)])]
    ppermute x19 -> x27, waiting for transfers between devices: 23.6 us -> 27.6 us  [swap(): return lax.ppermute(value, axis, [(i, i ^ bit) for i in range(count)])]
    convert_element_type x2 -> x4, other arithmetic: 3.96 us -> 7.53 us  [body(): sent = jnp.concatenate([sum((a[i:i + 1].astype(jnp.float32) for a, i in h...]
  transfers between devices with their start and end apart: 30 -> 38, of which waited for: 14 -> 12; matrix products, arithmetic and copies ran while one was open for 13% -> 10% of each run, Pallas kernels for 21% -> 20%
where the time goes in v2:
time: 231 us; the launch traced here: 230 us
  Pallas kernels  65.6 us (28%)
  waiting for transfers between devices  62.7 us (27%)
  starting transfers between devices  57.5 us (25%)
  other arithmetic  20.1 us (9%)
  matrix products  15.6 us (7%)
  local copies, waits for them, and re-layouts  7.68 us (3%)
    ppermute x9, waiting for transfers between devices, rotate(): lax.ppermute(value, axis, [(i, (i + steps) % count) for i in range(count)])  31.9 us
    ppermute x27, waiting for transfers between devices, swap(): return lax.ppermute(value, axis, [(i, i ^ bit) for i in range(count)])  27.6 us
    ppermute x9, starting transfers between devices, rotate(): lax.ppermute(value, axis, [(i, (i + steps) % count) for i in range(count)])  26.2 us
    ppermute x27, starting transfers between devices, swap(): return lax.ppermute(value, axis, [(i, i ^ bit) for i in range(count)])  21.8 us
    pallas_call x2, Pallas kernels, project(): pl.pallas_call(functools.partial(project_kernel, turns=turns, slots=slots...  18.2 us
    pallas_call x2, Pallas kernels, grad_terms(): pl.pallas_call(functools.partial(terms_kernel, steps=steps), grid_spec=pl...  15.9 us
    pallas_call x2, Pallas kernels, attention(): pl.pallas_call(functools.partial(attention_kernel, block=block, group=gro...  14.1 us
    ppermute x2, starting transfers between devices, shift(): lax.ppermute(value, axis, [(i, i + steps) for i in range(count - steps)])  9.49 us
  transfers between devices with their start and end apart: 38, of which 12 were waited for; matrix products, arithmetic and copies ran while one was open for 10% of the time, Pallas kernels for 20%

profile of v2, /device:TPU:0, one launch (start us, length us, event | category | flops | bytes accessed | tf_op | source)
XLA Modules:
  0.0 230.1 jit_solution(4435161426785989701)
XLA Ops:
  1.5 4.1 %fusion = f32[512]{0:T(512)S(1)} fusion(bf16[512,5376]{1,0:T(8,128)(2,1)} %param.13), kind=kLoop, calls=%fused_computation.2 | loop fusion | flops 8257024 | bytes 5507072 | tf_op jit(solution)/shard_map/reduce_sum | solution.py:420
  7.6 3.0 %convolution_convert_fusion.2 = bf16[512,512]{1,0:T(8,128)(2,1)S(1)} fusion(bf16[512,5376]{1,0:T(8,128)(2,1)S(1)} %fusion.2, bf16[5376,512]{1,0:T(8,128)(2,1)S(1)} %bitcast.27), kind=kOutput, calls=%fused_computation.7 | convolution fusion | flops 2818834432 | bytes 11534336 | tf_op jit(solution)/shard_map/dot_general | solution.py:424
  10.6 5.7 %convolution_convert_fusion.1 = bf16[512,512]{1,0:T(8,128)(2,1)S(1)} fusion(bf16[512,5376]{1,0:T(8,128)(2,1)S(1)} %fusion.2, bf16[5376,512]{1,0:T(8,128)(2,1)} %param.17), kind=kOutput, calls=%fused_computation.6 | convolution fusion | flops 2818834432 | bytes 11534336 | tf_op jit(solution)/shard_map/dot_general | solution.py:425
  16.5 5.1 %collective-permute-start = (bf16[512,512]{1,0:T(8,128)(2,1)S(1)}, bf16[512,512]{1,0:T(8,128)(2,1)S(1)}, u32[]{:S(2)}, u32[]{:S(2)}) collective-permute-start(bf16[512,512]{1,0:T(8,128)(2,1)S(1)} %pad_maximum_fusion.1.k0_ref.v0_ref), channel_id=1, source_target_pairs={{0,8},{4,12},{8,16},{12,20},{16,24},{20,28},{1,9},{5,13},{9,17},{1... | collective-permute-start | bytes 1572872 | tf_op jit(solution)/shard_map/ppermute | solution.py:26
  22.5 6.9 %convolution_convert_fusion.q_ref = bf16[512,1024]{1,0:T(8,128)(2,1)} fusion(bf16[512,5376]{1,0:T(8,128)(2,1)S(1)} %fusion.2, bf16[5376,1024]{1,0:T(8,128)(2,1)S(1)} %bitcast.25), kind=kOutput, calls=%fused_computation.5 | convolution fusion | flops 5637668864 | bytes 17563648 | tf_op jit(solution)/shard_map/dot_general | solution.py:434
  29.3 3.2 %collective-permute-done.k2_ref.v2_ref = bf16[512,512]{1,0:T(8,128)(2,1)S(1)} collective-permute-done((bf16[512,512]{1,0:T(8,128)(2,1)S(1)}, bf16[512,512]{1,0:T(8,128)(2,1)S(1)}, u32[]{:S(2)}, u32[]{:S(2)}) %collective-permute-start) | collective-permute-done | bytes 524320 | tf_op jit(solution)/shard_map/ppermute | solution.py:26
  35.4 7.0 %attention.2 = (bf16[512,512]{1,0:T(8,128)(2,1)}, bf16[512,512]{1,0:T(8,128)(2,1)}) custom-call(s32[1]{0:T(128)} %bitcast.pos_ref, bf16[512,1024]{1,0:T(8,128)(2,1)} %convolution_convert_fusion.q_ref, bf16[512,512]{1,0:T(8,128)(2,1)} %copy-done.9, bf16[512,512]{1,0:T(8,128)(2,1)} %copy-done.18, bf16[512,512]{1,0:T(8,128)(2,1)} %copy-done.8, ...), custom_call_target="tpu_custom_call" | custom-call | flops 2684354560 | bytes 2621440 | tf_op jit(solution)/shard_map/attention/pallas_call | solution.py:134
  43.1 8.6 %lead.1 = (bf16[4,672,512]{2,1,0:T(8,128)(2,1)}, bf16[4,672,512]{2,1,0:T(8,128)(2,1)}) custom-call(s32[16]{0:T(128)} %pad_add_fusion.1.tab_ref, bf16[512,5376]{1,0:T(8,128)(2,1)} %cot_ref.1), custom_call_target="tpu_custom_call" | custom-call | flops 22020096 | bytes 11010048 | tf_op jit(solution)/shard_map/lead/pallas_call | solution.py:177
  51.9 1.9 fusion.6
  55.4 2.6 %collective-permute-start.11 = (bf16[128,1408]{1,0:T(8,128)(2,1)S(1)}, bf16[128,1408]{1,0:T(8,128)(2,1)S(1)}, u32[]{:S(2)}, u32[]{:S(2)}) collective-permute-start(bf16[128,1408]{1,0:T(8,128)(2,1)S(1)} %get-tuple-element.59), channel_id=1, source_target_pairs={{0,2},{1,3},{2,0},{3,1},{4,6},{5,7},{6,4},{7,5},{8,10},{9,11},{10,... | collective-permute-start | bytes 1081352 | tf_op jit(solution)/shard_map/ppermute | solution.py:31
  59.3 4.4 %collective-permute-start.5 = (bf16[512,512]{1,0:T(8,128)(2,1)}, bf16[512,512]{1,0:T(8,128)(2,1)S(1)}, u32[]{:S(2)}, u32[]{:S(2)}) collective-permute-start(bf16[512,512]{1,0:T(8,128)(2,1)} %pad_maximum_fusion.2.k0_ref.v0_ref), channel_id=1, source_target_pairs={{0,8},{4,12},{8,16},{12,20},{16,24},{20,28},{1,9},{5,13},{9,17},{1... | collective-permute-start | bytes 1572872 | tf_op jit(solution)/shard_map/ppermute | solution.py:26
  63.8 3.3 %collective-permute-done.10 = bf16[128,1408]{1,0:T(8,128)(2,1)S(1)} collective-permute-done((bf16[128,1408]{1,0:T(8,128)(2,1)S(1)}, bf16[128,1408]{1,0:T(8,128)(2,1)S(1)}, u32[]{:S(2)}, u32[]{:S(2)}) %collective-permute-start.10) | collective-permute-done | bytes 360480 | tf_op jit(solution)/shard_map/ppermute | solution.py:31
  67.1 14.9 %collective-permute-done.11 = bf16[128,1408]{1,0:T(8,128)(2,1)S(1)} collective-permute-done((bf16[128,1408]{1,0:T(8,128)(2,1)S(1)}, bf16[128,1408]{1,0:T(8,128)(2,1)S(1)}, u32[]{:S(2)}, u32[]{:S(2)}) %collective-permute-start.11) | collective-permute-done | bytes 360480 | tf_op jit(solution)/shard_map/ppermute | solution.py:31
  82.1 2.5 %collective-permute-start.13 = (bf16[3,128,1408]{2,1,0:T(8,128)(2,1)S(1)}, bf16[3,128,1408]{2,1,0:T(8,128)(2,1)S(1)}, u32[]{:S(2)}, u32[]{:S(2)}) collective-permute-start(bf16[3,128,1408]{2,1,0:T(8,128)(2,1)S(1)} %pad_maximum_fusion.refs_7_.refs_3_), channel_id=1, source_target_pairs={{0,8},{4,12},{8,0},{12,4},{16,24},{20,28},{24,16},{28,20},{1,9},{5... | collective-permute-start | bytes 3244040 | tf_op jit(solution)/shard_map/ppermute | solution.py:36
  89.4 8.2 %collective-permute-start.2 = (bf16[512,512]{1,0:T(8,128)(2,1)}, bf16[512,512]{1,0:T(8,128)(2,1)}, u32[]{:S(2)}, u32[]{:S(2)}) collective-permute-start(bf16[512,512]{1,0:T(8,128)(2,1)} %get-tuple-element.29.refs_0_), channel_id=1, source_target_pairs={{0,1},{1,2},{2,3},{3,0},{4,5},{5,6},{6,7},{7,4},{8,9},{9,10},{10,1... | collective-permute-start | bytes 1572872 | tf_op jit(solution)/shard_map/ppermute | solution.py:31
  97.6 11.0 %collective-permute-done.13.refs_8_.refs_4_ = bf16[3,128,1408]{2,1,0:T(8,128)(2,1)S(1)} collective-permute-done((bf16[3,128,1408]{2,1,0:T(8,128)(2,1)S(1)}, bf16[3,128,1408]{2,1,0:T(8,128)(2,1)S(1)}, u32[]{:S(2)}, u32[]{:S(2)}) %collective-permute-start.13) | collective-permute-done | bytes 1081376 | tf_op jit(solution)/shard_map/ppermute | solution.py:36
  111.7 7.0 %attention.3 = (bf16[512,512]{1,0:T(8,128)(2,1)}, bf16[512,512]{1,0:T(8,128)(2,1)}) custom-call(s32[1]{0:T(128)} %bitcast.pos_ref, bf16[512,1024]{1,0:T(8,128)(2,1)} %convolution_convert_fusion.q_ref, bf16[512,512]{1,0:T(8,128)(2,1)} %copy-done.7, bf16[512,512]{1,0:T(8,128)(2,1)} %copy-done.17, bf16[512,512]{1,0:T(8,128)(2,1)} %pad_maximum_fusion.2.k0_ref.v0_ref, ...), custom_call_target="tpu_custom_call" | custom-call | flops 2684354560 | bytes 2621440 | tf_op jit(solution)/shard_map/attention/pallas_call | solution.py:134
  118.7 8.3 %collective-permute-start.7 = (bf16[512,512]{1,0:T(8,128)(2,1)}, bf16[512,512]{1,0:T(8,128)(2,1)}, u32[]{:S(2)}, u32[]{:S(2)}) collective-permute-start(bf16[512,512]{1,0:T(8,128)(2,1)} %get-tuple-element.31.refs_1_), channel_id=1, source_target_pairs={{0,1},{1,2},{2,3},{3,0},{4,5},{5,6},{6,7},{7,4},{8,9},{9,10},{10,1... | collective-permute-start | bytes 1572872 | tf_op jit(solution)/shard_map/ppermute | solution.py:31
  127.8 7.9 %grad_terms.2 = (bf16[2,672,256]{2,1,0:T(8,128)(2,1)}, bf16[2,672,256]{2,1,0:T(8,128)(2,1)}, bf16[2,672,256]{2,1,0:T(8,128)(2,1)}, bf16[2,672,256]{2,1,0:T(8,128)(2,1)}) custom-call(s32[28]{0:T(128)} %pad_add_fusion.tab_ref, bf16[4,672,512]{2,1,0:T(8,128)(2,1)} %get-tuple-element.37.cot0_ref, bf16[4,672,512]{2,1,0:T(8,128)(2,1)} %collective-permute-done.20.cot1_ref, ...), custom_call_target="tpu_custom_call" | custom-call | flops 2818572288 | bytes 8257536 | tf_op jit(solution)/shard_map/grad_terms/pallas_call | solution.py:237
  137.3 3.4 %collective-permute-done.7.refs_3_ = bf16[512,512]{1,0:T(8,128)(2,1)} collective-permute-done((bf16[512,512]{1,0:T(8,128)(2,1)}, bf16[512,512]{1,0:T(8,128)(2,1)}, u32[]{:S(2)}, u32[]{:S(2)}) %collective-permute-start.7) | collective-permute-done | bytes 524320 | tf_op jit(solution)/shard_map/ppermute | solution.py:31
  142.7 8.0 %grad_terms.3 = (bf16[2,672,256]{2,1,0:T(8,128)(2,1)}, bf16[2,672,256]{2,1,0:T(8,128)(2,1)}, bf16[2,672,256]{2,1,0:T(8,128)(2,1)}, bf16[2,672,256]{2,1,0:T(8,128)(2,1)}) custom-call(s32[28]{0:T(128)} %pad_add_fusion.tab_ref, bf16[4,672,512]{2,1,0:T(8,128)(2,1)} %get-tuple-element.37.cot0_ref, bf16[4,672,512]{2,1,0:T(8,128)(2,1)} %collective-permute-done.20.cot1_ref, ...), custom_call_target="tpu_custom_call" | custom-call | flops 2818572288 | bytes 8257536 | tf_op jit(solution)/shard_map/grad_terms/pallas_call | solution.py:237
  153.4 9.1 %collective-permute-done.8.refs_5_ = bf16[512,512]{1,0:T(8,128)(2,1)} collective-permute-done((bf16[512,512]{1,0:T(8,128)(2,1)}, bf16[512,512]{1,0:T(8,128)(2,1)}, u32[]{:S(2)}, u32[]{:S(2)}) %collective-permute-start.8) | collective-permute-done | bytes 524320 | tf_op jit(solution)/shard_map/ppermute | solution.py:31
  164.3 3.8 %turned.1.refs_12_ = bf16[672,1024]{1,0:T(8,128)(2,1)} custom-call(s32[5]{0:T(128)} %stack.35.pos_ref, bf16[1024,5376]{1,0:T(8,128)(2,1)} %w_ref.1), custom_call_target="tpu_custom_call" | custom-call | tf_op jit(solution)/shard_map/turned/pallas_call | solution.py:381
  168.8 1.9 add_convert_fusion.3
  172.0 1.9 add_convert_fusion.2
  173.9 1.9 add_convert_fusion.1
  175.8 10.4 %collective-permute-done.29.refs_10_ = bf16[2,672,256]{2,1,0:T(8,128)(2,1)S(1)} collective-permute-done((bf16[2,672,256]{2,1,0:T(8,128)(2,1)}, bf16[2,672,256]{2,1,0:T(8,128)(2,1)S(1)}, u32[]{:S(2)}, u32[]{:S(2)}) %collective-permute-start.29) | collective-permute-done | bytes 688160 | tf_op jit(solution)/shard_map/ppermute | solution.py:36
  193.4 10.9 %project.2.refs_2_ = f32[512,1408]{1,0:T(8,128)} custom-call(s32[5]{0:T(128)} %stack.35.pos_ref, bf16[512,512]{1,0:T(8,128)(2,1)} %get-tuple-element.29.refs_0_, bf16[512,512]{1,0:T(8,128)(2,1)} %get-tuple-element.31.refs_1_, bf16[512,512]{1,0:T(8,128)(2,1)} %collective-permute-done.2.refs_2_, bf16[512,512]{1,0:T(8,128)(2,1)} %collective-permute-done.7.refs_3_, ...), custom_call_target="tpu_custom_call" | custom-call | flops 4429185024 | bytes 17563648 | tf_op jit(solution)/shard_map/project/pallas_call | solution.py:308
  204.3 7.3 %project.3 = bf16[512,1344]{1,0:T(8,128)(2,1)} custom-call(s32[5]{0:T(128)} %stack.35.pos_ref, bf16[512,512]{1,0:T(8,128)(2,1)} %collective-permute-done.4.refs_0_, bf16[512,512]{1,0:T(8,128)(2,1)} %collective-permute-done.9.refs_1_, f32[512,1408]{1,0:T(8,128)} %project.2.refs_2_, bf16[3,128,1408]{2,1,0:T(8,128)(2,1)} %copy-done.1, ...), custom_call_target="tpu_custom_call" | custom-call | flops 1476395008 | bytes 9699328 | tf_op jit(solution)/shard_map/project/pallas_call | solution.py:308
  211.6 2.5 %copy.18 = bf16[512,1344]{0,1:T(8,128)(2,1)} copy(bf16[512,1344]{1,0:T(8,128)(2,1)} %project.3) | data formatting | bytes 2752512
  215.8 4.9 %finish.1 = (f32[672,1024]{1,0:T(8,128)}, f32[1,1024]{1,0:T(1,128)}) custom-call(bf16[2,672,256]{2,1,0:T(8,128)(2,1)} %get-tuple-element.39.refs_0_, bf16[2,672,256]{2,1,0:T(8,128)(2,1)} %collective-permute-done.22.refs_1_, bf16[1,672,256]{2,1,0:T(8,128)(2,1)} %copy-done.10, bf16[2,672,256]{2,1,0:T(8,128)(2,1)} %get-tuple-element.41.refs_3_, ...), custom_call_target="tpu_custom_call" | custom-call | flops 5505024 | bytes 8257536 | tf_op jit(solution)/shard_map/finish/pallas_call | solution.py:352
  223.7 2.4 %collective-permute-start.35 = (f32[8]{0:T(128)S(1)}, f32[8]{0:T(128)S(1)}, u32[]{:S(2)}, u32[]{:S(2)}) collective-permute-start(f32[8]{0:T(128)S(1)} %reduce_sum.19), channel_id=1, source_target_pairs={{0,20},{4,16},{8,28},{12,24},{16,4},{20,0},{24,12},{28,8},{1,21},{... | collective-permute-start | bytes 104 | tf_op jit(solution)/shard_map/ppermute | solution.py:36
  (138 shorter events, 44.8 us)
Async XLA Ops:
  16.5 16.0 %collective-permute-start = (bf16[512,512]{1,0:T(8,128)(2,1)S(1)}, bf16[512,512]{1,0:T(8,128)(2,1)S(1)}, u32[]{:S(2)}, u32[]{:S(2)}) collective-permute-start(bf16[512,512]{1,0:T(8,128)(2,1)S(1)} %pad_maximum_fusion.1.k0_ref.v0_ref), channel_id=1, source_target_pairs={{0,8},{4,12},{8,16},{12,20},{16,24},{20,28},{1,9},{5,13},{9,17},{1... | collective-permute-start | bytes 1572872 | tf_op jit(solution)/shard_map/ppermute | solution.py:26
  51.7 76.0 %collective-permute-start.20 = (bf16[4,672,512]{2,1,0:T(8,128)(2,1)}, bf16[4,672,512]{2,1,0:T(8,128)(2,1)}, u32[]{:S(2)}, u32[]{:S(2)}) collective-permute-start(bf16[4,672,512]{2,1,0:T(8,128)(2,1)} %get-tuple-element.38), channel_id=1, source_target_pairs={{0,4},{4,0},{8,12},{12,8},{16,20},{20,16},{24,28},{28,24},{1,5},{5... | collective-permute-start | bytes 8257544 | tf_op jit(solution)/shard_map/ppermute | solution.py:36
  53.8 13.3 %collective-permute-start.10 = (bf16[128,1408]{1,0:T(8,128)(2,1)S(1)}, bf16[128,1408]{1,0:T(8,128)(2,1)S(1)}, u32[]{:S(2)}, u32[]{:S(2)}) collective-permute-start(bf16[128,1408]{1,0:T(8,128)(2,1)S(1)} %get-tuple-element.60), channel_id=1, source_target_pairs={{0,1},{1,2},{2,3},{3,0},{4,5},{5,6},{6,7},{7,4},{8,9},{9,10},{10,1... | collective-permute-start | bytes 1081352 | tf_op jit(solution)/shard_map/ppermute | solution.py:31
  55.4 26.6 %collective-permute-start.11 = (bf16[128,1408]{1,0:T(8,128)(2,1)S(1)}, bf16[128,1408]{1,0:T(8,128)(2,1)S(1)}, u32[]{:S(2)}, u32[]{:S(2)}) collective-permute-start(bf16[128,1408]{1,0:T(8,128)(2,1)S(1)} %get-tuple-element.59), channel_id=1, source_target_pairs={{0,2},{1,3},{2,0},{3,1},{4,6},{5,7},{6,4},{7,5},{8,10},{9,11},{10,... | collective-permute-start | bytes 1081352 | tf_op jit(solution)/shard_map/ppermute | solution.py:31
  58.0 24.0 %collective-permute-start.12 = (bf16[128,1408]{1,0:T(8,128)(2,1)S(1)}, bf16[128,1408]{1,0:T(8,128)(2,1)S(1)}, u32[]{:S(2)}, u32[]{:S(2)}) collective-permute-start(bf16[128,1408]{1,0:T(8,128)(2,1)S(1)} %get-tuple-element.58), channel_id=1, source_target_pairs={{0,3},{1,0},{2,1},{3,2},{4,7},{5,4},{6,5},{7,6},{8,11},{9,8},{10,9... | collective-permute-start | bytes 1081352 | tf_op jit(solution)/shard_map/ppermute | solution.py:31
  59.3 26.9 %collective-permute-start.5 = (bf16[512,512]{1,0:T(8,128)(2,1)}, bf16[512,512]{1,0:T(8,128)(2,1)S(1)}, u32[]{:S(2)}, u32[]{:S(2)}) collective-permute-start(bf16[512,512]{1,0:T(8,128)(2,1)} %pad_maximum_fusion.2.k0_ref.v0_ref), channel_id=1, source_target_pairs={{0,8},{4,12},{8,16},{12,20},{16,24},{20,28},{1,9},{5,13},{9,17},{1... | collective-permute-start | bytes 1572872 | tf_op jit(solution)/shard_map/ppermute | solution.py:26
  82.1 26.5 %collective-permute-start.13 = (bf16[3,128,1408]{2,1,0:T(8,128)(2,1)S(1)}, bf16[3,128,1408]{2,1,0:T(8,128)(2,1)S(1)}, u32[]{:S(2)}, u32[]{:S(2)}) collective-permute-start(bf16[3,128,1408]{2,1,0:T(8,128)(2,1)S(1)} %pad_maximum_fusion.refs_7_.refs_3_), channel_id=1, source_target_pairs={{0,8},{4,12},{8,0},{12,4},{16,24},{20,28},{24,16},{28,20},{1,9},{5... | collective-permute-start | bytes 3244040 | tf_op jit(solution)/shard_map/ppermute | solution.py:36
  84.7 25.4 %collective-permute-start.14 = (bf16[3,128,1408]{2,1,0:T(8,128)(2,1)S(1)}, bf16[3,128,1408]{2,1,0:T(8,128)(2,1)S(1)}, u32[]{:S(2)}, u32[]{:S(2)}) collective-permute-start(bf16[3,128,1408]{2,1,0:T(8,128)(2,1)S(1)} %pad_maximum_fusion.refs_7_.refs_3_), channel_id=1, source_target_pairs={{0,16},{4,20},{8,24},{12,28},{16,0},{20,4},{24,8},{28,12},{1,17},{... | collective-permute-start | bytes 3244040 | tf_op jit(solution)/shard_map/ppermute | solution.py:36
  87.5 48.2 %collective-permute-start.16 = (bf16[3,128,1408]{2,1,0:T(8,128)(2,1)S(1)}, bf16[3,128,1408]{2,1,0:T(8,128)(2,1)}, u32[]{:S(2)}, u32[]{:S(2)}) collective-permute-start(bf16[3,128,1408]{2,1,0:T(8,128)(2,1)S(1)} %pad_maximum_fusion.refs_7_.refs_3_), channel_id=1, source_target_pairs={{0,4},{4,0},{8,12},{12,8},{16,20},{20,16},{24,28},{28,24},{1,5},{5... | collective-permute-start | bytes 3244040 | tf_op jit(solution)/shard_map/ppermute | solution.py:36
  89.4 29.3 %collective-permute-start.2 = (bf16[512,512]{1,0:T(8,128)(2,1)}, bf16[512,512]{1,0:T(8,128)(2,1)}, u32[]{:S(2)}, u32[]{:S(2)}) collective-permute-start(bf16[512,512]{1,0:T(8,128)(2,1)} %get-tuple-element.29.refs_0_), channel_id=1, source_target_pairs={{0,1},{1,2},{2,3},{3,0},{4,5},{5,6},{6,7},{7,4},{8,9},{9,10},{10,1... | collective-permute-start | bytes 1572872 | tf_op jit(solution)/shard_map/ppermute | solution.py:31
  108.7 18.4 %collective-permute-start.21 = (bf16[512,512]{1,0:T(8,128)(2,1)}, bf16[512,512]{1,0:T(8,128)(2,1)}, u32[]{:S(2)}, u32[]{:S(2)}) collective-permute-start(bf16[512,512]{1,0:T(8,128)(2,1)} %get-tuple-element.35.att0_ref), channel_id=1, source_target_pairs={{0,4},{4,0},{8,12},{12,8},{16,20},{20,16},{24,28},{28,24},{1,5},{5... | collective-permute-start | bytes 1572872 | tf_op jit(solution)/shard_map/ppermute | solution.py:36
  110.1 52.3 %collective-permute-start.15 = (bf16[3,128,1408]{2,1,0:T(8,128)(2,1)S(1)}, bf16[3,128,1408]{2,1,0:T(8,128)(2,1)}, u32[]{:S(2)}, u32[]{:S(2)}) collective-permute-start(bf16[3,128,1408]{2,1,0:T(8,128)(2,1)S(1)} %collective-permute-done.13.refs_8_.refs_4_), channel_id=1, source_target_pairs={{0,16},{4,20},{8,24},{12,28},{16,0},{20,4},{24,8},{28,12},{1,17},{... | collective-permute-start | bytes 3244040 | tf_op jit(solution)/shard_map/ppermute | solution.py:36
  118.7 21.9 %collective-permute-start.7 = (bf16[512,512]{1,0:T(8,128)(2,1)}, bf16[512,512]{1,0:T(8,128)(2,1)}, u32[]{:S(2)}, u32[]{:S(2)}) collective-permute-start(bf16[512,512]{1,0:T(8,128)(2,1)} %get-tuple-element.31.refs_1_), channel_id=1, source_target_pairs={{0,1},{1,2},{2,3},{3,0},{4,5},{5,6},{6,7},{7,4},{8,9},{9,10},{10,1... | collective-permute-start | bytes 1572872 | tf_op jit(solution)/shard_map/ppermute | solution.py:31
  127.1 15.1 %collective-permute-start.26 = (bf16[512,512]{1,0:T(8,128)(2,1)}, bf16[512,512]{1,0:T(8,128)(2,1)}, u32[]{:S(2)}, u32[]{:S(2)}) collective-permute-start(bf16[512,512]{1,0:T(8,128)(2,1)} %get-tuple-element.43.att0_ref), channel_id=1, source_target_pairs={{0,4},{4,0},{8,12},{12,8},{16,20},{20,16},{24,28},{28,24},{1,5},{5... | collective-permute-start | bytes 1572872 | tf_op jit(solution)/shard_map/ppermute | solution.py:36
  127.7 24.2 %collective-permute-start.3 = (bf16[512,512]{1,0:T(8,128)(2,1)}, bf16[512,512]{1,0:T(8,128)(2,1)}, u32[]{:S(2)}, u32[]{:S(2)}) collective-permute-start(bf16[512,512]{1,0:T(8,128)(2,1)} %collective-permute-done.2.refs_2_), channel_id=1, source_target_pairs={{0,1},{1,2},{2,3},{3,0},{4,5},{5,6},{6,7},{7,4},{8,9},{9,10},{10,1... | collective-permute-start | bytes 1572872 | tf_op jit(solution)/shard_map/ppermute | solution.py:31
  135.8 27.2 %collective-permute-start.22 = (bf16[2,672,256]{2,1,0:T(8,128)(2,1)}, bf16[2,672,256]{2,1,0:T(8,128)(2,1)}, u32[]{:S(2)}, u32[]{:S(2)}) collective-permute-start(bf16[2,672,256]{2,1,0:T(8,128)(2,1)} %get-tuple-element.40), channel_id=1, source_target_pairs={{0,8},{4,12},{8,0},{12,4},{16,24},{20,28},{24,16},{28,20},{1,9},{5... | collective-permute-start | bytes 2064392 | tf_op jit(solution)/shard_map/ppermute | solution.py:36
  140.7 21.8 %collective-permute-start.8 = (bf16[512,512]{1,0:T(8,128)(2,1)}, bf16[512,512]{1,0:T(8,128)(2,1)}, u32[]{:S(2)}, u32[]{:S(2)}) collective-permute-start(bf16[512,512]{1,0:T(8,128)(2,1)} %collective-permute-done.7.refs_3_), channel_id=1, source_target_pairs={{0,1},{1,2},{2,3},{3,0},{4,5},{5,6},{6,7},{7,4},{8,9},{9,10},{10,1... | collective-permute-start | bytes 1572872 | tf_op jit(solution)/shard_map/ppermute | solution.py:31
  142.2 26.0 %collective-permute-start.24 = (bf16[2,672,256]{2,1,0:T(8,128)(2,1)}, bf16[2,672,256]{2,1,0:T(8,128)(2,1)}, u32[]{:S(2)}, u32[]{:S(2)}) collective-permute-start(bf16[2,672,256]{2,1,0:T(8,128)(2,1)} %get-tuple-element.42), channel_id=1, source_target_pairs={{0,16},{4,20},{8,24},{12,28},{16,0},{20,4},{24,8},{28,12},{1,17},{... | collective-permute-start | bytes 2064392 | tf_op jit(solution)/shard_map/ppermute | solution.py:36
  151.9 18.8 %collective-permute-start.27 = (bf16[2,672,256]{2,1,0:T(8,128)(2,1)}, bf16[2,672,256]{2,1,0:T(8,128)(2,1)}, u32[]{:S(2)}, u32[]{:S(2)}) collective-permute-start(bf16[2,672,256]{2,1,0:T(8,128)(2,1)} %get-tuple-element.45), channel_id=1, source_target_pairs={{0,8},{4,12},{8,0},{12,4},{16,24},{20,28},{24,16},{28,20},{1,9},{5... | collective-permute-start | bytes 2064392 | tf_op jit(solution)/shard_map/ppermute | solution.py:36
  162.5 26.8 %collective-permute-start.17 = (bf16[3,128,1408]{2,1,0:T(8,128)(2,1)S(1)}, bf16[3,128,1408]{2,1,0:T(8,128)(2,1)S(1)}, u32[]{:S(2)}, u32[]{:S(2)}) collective-permute-start(bf16[3,128,1408]{2,1,0:T(8,128)(2,1)S(1)} %collective-permute-done.13.refs_8_.refs_4_), channel_id=1, source_target_pairs={{0,4},{4,0},{8,12},{12,8},{16,20},{20,16},{24,28},{28,24},{1,5},{5... | collective-permute-start | bytes 3244040 | tf_op jit(solution)/shard_map/ppermute | solution.py:36
  162.5 27.4 %collective-permute-start.18 = (bf16[3,128,1408]{2,1,0:T(8,128)(2,1)S(1)}, bf16[3,128,1408]{2,1,0:T(8,128)(2,1)}, u32[]{:S(2)}, u32[]{:S(2)}) collective-permute-start(bf16[3,128,1408]{2,1,0:T(8,128)(2,1)S(1)} %collective-permute-done.14.refs_9_.refs_5_), channel_id=1, source_target_pairs={{0,4},{4,0},{8,12},{12,8},{16,20},{20,16},{24,28},{28,24},{1,5},{5... | collective-permute-start | bytes 3244040 | tf_op jit(solution)/shard_map/ppermute | solution.py:36
  163.0 28.9 %collective-permute-start.19 = (bf16[3,128,1408]{2,1,0:T(8,128)(2,1)}, bf16[3,128,1408]{2,1,0:T(8,128)(2,1)}, u32[]{:S(2)}, u32[]{:S(2)}) collective-permute-start(bf16[3,128,1408]{2,1,0:T(8,128)(2,1)} %collective-permute-done.15.refs_10_.refs_6_), channel_id=1, source_target_pairs={{0,4},{4,0},{8,12},{12,8},{16,20},{20,16},{24,28},{28,24},{1,5},{5... | collective-permute-start | bytes 3244040 | tf_op jit(solution)/shard_map/ppermute | solution.py:36
  168.2 18.0 %collective-permute-start.29 = (bf16[2,672,256]{2,1,0:T(8,128)(2,1)}, bf16[2,672,256]{2,1,0:T(8,128)(2,1)S(1)}, u32[]{:S(2)}, u32[]{:S(2)}) collective-permute-start(bf16[2,672,256]{2,1,0:T(8,128)(2,1)} %get-tuple-element.47), channel_id=1, source_target_pairs={{0,16},{4,20},{8,24},{12,28},{16,0},{20,4},{24,8},{28,12},{1,17},{... | collective-permute-start | bytes 2064392 | tf_op jit(solution)/shard_map/ppermute | solution.py:36
  170.7 19.7 %collective-permute-start.4 = (bf16[512,512]{1,0:T(8,128)(2,1)}, bf16[512,512]{1,0:T(8,128)(2,1)}, u32[]{:S(2)}, u32[]{:S(2)}) collective-permute-start(bf16[512,512]{1,0:T(8,128)(2,1)} %collective-permute-done.3.refs_4_), channel_id=1, source_target_pairs={{0,1},{1,2},{2,3},{3,0},{4,5},{5,6},{6,7},{7,4},{8,9},{9,10},{10,1... | collective-permute-start | bytes 1572872 | tf_op jit(solution)/shard_map/ppermute | solution.py:31
  186.2 18.1 %collective-permute-start.9 = (bf16[512,512]{1,0:T(8,128)(2,1)}, bf16[512,512]{1,0:T(8,128)(2,1)}, u32[]{:S(2)}, u32[]{:S(2)}) collective-permute-start(bf16[512,512]{1,0:T(8,128)(2,1)} %collective-permute-done.8.refs_5_), channel_id=1, source_target_pairs={{0,1},{1,2},{2,3},{3,0},{4,5},{5,6},{6,7},{7,4},{8,9},{9,10},{10,1... | collective-permute-start | bytes 1572872 | tf_op jit(solution)/shard_map/ppermute | solution.py:31
  189.3 24.8 %collective-permute-start.23 = (bf16[1,672,256]{2,1,0:T(8,128)(2,1)}, bf16[1,672,256]{2,1,0:T(8,128)(2,1)S(1)}, u32[]{:S(2)}, u32[]{:S(2)}) collective-permute-start(bf16[1,672,256]{2,1,0:T(8,128)(2,1)} %add_convert_fusion.3), channel_id=1, source_target_pairs={{0,16},{4,20},{8,24},{12,28},{16,0},{20,4},{24,8},{28,12},{1,17},{... | collective-permute-start | bytes 1032200 | tf_op jit(solution)/shard_map/ppermute | solution.py:36
  189.9 24.2 %collective-permute-start.25 = (bf16[1,672,256]{2,1,0:T(8,128)(2,1)}, bf16[1,672,256]{2,1,0:T(8,128)(2,1)S(1)}, u32[]{:S(2)}, u32[]{:S(2)}) collective-permute-start(bf16[1,672,256]{2,1,0:T(8,128)(2,1)} %add_convert_fusion.2), channel_id=1, source_target_pairs={{0,8},{4,12},{8,0},{12,4},{16,24},{20,28},{24,16},{28,20},{1,9},{5... | collective-permute-start | bytes 1032200 | tf_op jit(solution)/shard_map/ppermute | solution.py:36
  190.4 23.7 %collective-permute-start.28 = (bf16[1,672,256]{2,1,0:T(8,128)(2,1)}, bf16[1,672,256]{2,1,0:T(8,128)(2,1)S(1)}, u32[]{:S(2)}, u32[]{:S(2)}) collective-permute-start(bf16[1,672,256]{2,1,0:T(8,128)(2,1)} %add_convert_fusion.1), channel_id=1, source_target_pairs={{0,16},{4,20},{8,24},{12,28},{16,0},{20,4},{24,8},{28,12},{1,17},{... | collective-permute-start | bytes 1032200 | tf_op jit(solution)/shard_map/ppermute | solution.py:36
  191.9 22.2 %collective-permute-start.30 = (bf16[1,672,256]{2,1,0:T(8,128)(2,1)}, bf16[1,672,256]{2,1,0:T(8,128)(2,1)S(1)}, u32[]{:S(2)}, u32[]{:S(2)}) collective-permute-start(bf16[1,672,256]{2,1,0:T(8,128)(2,1)} %add_convert_fusion), channel_id=1, source_target_pairs={{0,8},{4,12},{8,0},{12,4},{16,24},{20,28},{24,16},{28,20},{1,9},{5... | collective-permute-start | bytes 1032200 | tf_op jit(solution)/shard_map/ppermute | solution.py:36
  221.6 5.0 %collective-permute-start.36 = (f32[8]{0:T(128)S(1)}, f32[8]{0:T(128)S(1)}, u32[]{:S(2)}, u32[]{:S(2)}) collective-permute-start(f32[8]{0:T(128)S(1)} %reduce_sum.19), channel_id=1, source_target_pairs={{0,24},{4,28},{8,16},{12,20},{16,8},{20,12},{24,0},{28,4},{1,25},{... | collective-permute-start | bytes 104 | tf_op jit(solution)/shard_map/ppermute | solution.py:36
  222.2 6.0 %collective-permute-start.34 = (f32[8]{0:T(128)S(1)}, f32[8]{0:T(128)S(1)}, u32[]{:S(2)}, u32[]{:S(2)}) collective-permute-start(f32[8]{0:T(128)S(1)} %reduce_sum.19), channel_id=1, source_target_pairs={{0,16},{4,20},{8,24},{12,28},{16,0},{20,4},{24,8},{28,12},{1,17},{... | collective-permute-start | bytes 104 | tf_op jit(solution)/shard_map/ppermute | solution.py:36
  223.7 4.5 %collective-permute-start.35 = (f32[8]{0:T(128)S(1)}, f32[8]{0:T(128)S(1)}, u32[]{:S(2)}, u32[]{:S(2)}) collective-permute-start(f32[8]{0:T(128)S(1)} %reduce_sum.19), channel_id=1, source_target_pairs={{0,20},{4,16},{8,28},{12,24},{16,4},{20,0},{24,12},{28,8},{1,21},{... | collective-permute-start | bytes 104 | tf_op jit(solution)/shard_map/ppermute | solution.py:36
  (32 other events, 450.9 us)

commit v3 on v2

--- a/solution.py
+++ b/solution.py
@@ -122,13 +122,14 @@
 
 def attention(position, queries, kv2, kv1, kv0, gate_row, side):
     rows = queries.shape[0]
-    kv_heads = kv0.shape[1] // (2 * HEAD_SIZE)
+    all_heads = kv0.shape[1] // (2 * HEAD_SIZE)
+    kv_heads = all_heads // 2
     wide = queries.shape[1] // (2 * kv_heads)
     group = wide // HEAD_SIZE
     width = kv_heads * wide
     block = math.gcd(rows, 256)
-    key_spec = pl.BlockSpec((rows, HEAD_SIZE), lambda h, pos: (0, h))
-    value_spec = pl.BlockSpec((rows, HEAD_SIZE), lambda h, pos: (0, kv_heads + h))
+    key_spec = pl.BlockSpec((rows, HEAD_SIZE), lambda h, pos: (0, side * kv_heads + h))
+    value_spec = pl.BlockSpec((rows, HEAD_SIZE), lambda h, pos: (0, all_heads + side * kv_heads + h))
     query_spec = pl.BlockSpec((rows, wide), lambda h, pos: (0, side * kv_heads + h))
     out_spec = pl.BlockSpec((rows, wide), lambda h, pos: (0, h))
     return pl.pallas_call(
@@ -264,7 +265,7 @@
     base_ref = rest.pop(0) if turns[0] != -1 else None
     own_ref = rest.pop(0) if turns[0] == -1 else None
     w_refs = rest[:len(slots)]
-    out_ref, weight, sems = rest[len(slots):]
+    out_ref, weight, flipped, sems = rest[len(slots):]
     position = pos_ref[0]
     copies = []
     for k, turn in enumerate(turns):
@@ -294,9 +295,10 @@
             )
             total = part if total is None else total + part
     if final:
-        wide = total.shape[1]
-        total = pltpu.roll(total, lax.rem(wide - pos_ref[2], wide), 1)[:, :out_ref.shape[1]]
-    out_ref[...] = total.astype(out_ref.dtype)
+        flipped[...] = total.astype(flipped.dtype).T
+        out_ref[...] = flipped[pl.ds(pl.multiple_of(pos_ref[2], 16), out_ref.shape[0])]
+    else:
+        out_ref[...] = total
 
 
 def project(position, xs, base, own, weights, slots, turns, out_cols, dtype):
@@ -311,9 +313,11 @@
         in_specs=[pl.BlockSpec(memory_space=pltpu.SMEM)] + [whole] * len(xs)
         + [anywhere if base is None else whole] + [anywhere] * len(weights),
         out_specs=whole,
-        out_shape=jax.ShapeDtypeStruct((rows, out_cols), dtype),
+        out_shape=jax.ShapeDtypeStruct(
+            (rows, out_cols) if base is None else (out_cols, rows), dtype),
         scratch_shapes=[
             pltpu.VMEM((len(turns), 2 * middle, cols), jnp.bfloat16),
+            pltpu.VMEM((cols, rows) if base is not None else (16, 128), jnp.bfloat16),
             pltpu.SemaphoreType.DMA((len(turns), len(slots))),
         ],
         cost_estimate=pl.CostEstimate(
@@ -424,15 +428,10 @@
     keys = jnp.dot(normed, w_key, preferred_element_type=jnp.float32).astype(jnp.bfloat16)
     values = jnp.dot(normed, value_weight, preferred_element_type=jnp.float32).astype(
         jnp.bfloat16)
-    kv_half = keys.shape[1] // 2
-    kv_sides = []
-    kv2_sides = []
-    for h in range(2):
-        cols = slice(h * kv_half, (h + 1) * kv_half)
-        kv_sides.append(jnp.concatenate([keys[:, cols], values[:, cols]], axis=1))
-        kv2_sides.append(shift(kv_sides[h], "ctx", 2))
+    kv0 = jnp.concatenate([keys, values], axis=1)
+    kv2 = shift(kv0, "ctx", 2)
     queries = jnp.dot(
-        after(normed, *kv_sides), w_query, preferred_element_type=jnp.float32
+        after(normed, kv0), w_query, preferred_element_type=jnp.float32
     ).astype(jnp.bfloat16)
 
     gate_value, gate_slope, penalty_term = hard_concrete(mask_logit, noise_draw)
@@ -445,26 +444,25 @@
         for relative in list(parts):
             parts[relative | bit] = swap(parts[relative], "ctx", bit)
 
-    mixed = [jnp.where(p % 2 == 0, kv_sides[h], after(kv2_sides[h], queries)) for h in range(2)]
+    leaving, cot_home = lead_blocks(after(p % 2, own_part), cotangent, n_ctx)
+    cot_other = swap(leaving, "ctx", 1)
+    mixed = jnp.where(p % 2 == 0, kv0, after(kv2, cot_home))
+    kv1 = swap(mixed, "ctx", 1)
+    w_mine = turned(after(scalars, mixed), w_out, own_cols)
 
     attended = []
     moving = []
     others = []
     for h in range(2):
-        kv1 = swap(mixed[h], "ctx", 1)
         att, gat = attention(
-            position, queries, kv2_sides[h], kv1, kv_sides[h], gate_row, h)
+            position, queries, kv2, kv1, kv0, gate_row, h)
         attended.append(att)
         chain = [gat]
         for _ in range(1, n_head):
             chain.append(rotate(chain[-1], "head", 1))
         moving.append(chain)
         others.append(swap(att, "ctx", 1))
-        if h == 0:
-            leaving, cot_home = lead_blocks(after(p % 2, att), cotangent, n_ctx)
-            cot_other = swap(leaving, "ctx", 1)
-
-    w_mine = turned(after(scalars, attended[1]), w_out, own_cols)
+
 
     grads = []
     relative = [2 * j for j in range(n_ctx // 2)]
@@ -495,24 +493,21 @@
     slots = tuple(parts)
     weights = [parts[r] for r in slots]
 
-    early = list(range(n_head - 2))
-    xs = [moving[h][0] for h in range(2)]
-    for t in early:
-        xs += [moving[h][t + 1] for h in range(2)]
-    base = project(scalars, xs, None, w_out, weights, slots, (-1,) + tuple(early),
-                   wide_cols, jnp.float32)
-    layer_out = project(scalars, [moving[h][-1] for h in range(2)], base, None, weights,
-                        slots, (n_head - 2,), out_cols, jnp.bfloat16)
+    late = tuple(range(max(n_head - 3, 0), n_head - 1))
+    early = tuple(range(late[0]))
+    pairs = [[moving[h][t + 1] for h in range(2)] for t in range(n_head - 1)]
+    xs = [moving[h][0] for h in range(2)] + sum((pairs[t] for t in early), [])
+    base = project(scalars, xs, None, w_out, weights, slots, (-1,) + early, wide_cols,
+                   jnp.float32)
+    layer_out = project(scalars, sum((pairs[t] for t in late), []), base, None, weights,
+                        slots, late, out_cols, jnp.bfloat16).T
 
     grad_columns, products = finish(grads, w_mine, gate_row * inv_root)
     grad_out_proj = grad_columns.T
     head_terms = jnp.sum(products.reshape(local_heads, HEAD_SIZE), axis=1)
-    values = [head_terms]
-    for member in range(1, n_ctx):
-        values.append(swap(head_terms, "ctx", member))
-    while len(values) > 1:
-        values = [values[i] + values[i + 1] for i in range(0, len(values), 2)]
-    grad_logit = values[0] * inv_root * gate_slope + penalty_term
+    for bit in [1] + bits:
+        head_terms = head_terms + swap(head_terms, "ctx", bit)
+    grad_logit = head_terms * inv_root * gate_slope + penalty_term
     return (layer_out, grad_logit, grad_out_proj)
 
 

time: 231 us -> 202 us (0.87)
  starting transfers between devices: 57.5 us -> 28 us
  waiting for transfers between devices: 62.7 us -> 66.4 us
    ppermute x9, starting transfers between devices: 26.2 us -> 8.15 us  [rotate(): lax.ppermute(value, axis, [(i, (i + steps) % count) for i in range(count)])]
    ppermute x27 -> x22, starting transfers between devices: 21.8 us -> 15.5 us  [swap(): return lax.ppermute(value, axis, [(i, i ^ bit) for i in range(count)])]
    ppermute x27 -> x22, waiting for transfers between devices: 27.6 us -> 32.9 us  [swap(): return lax.ppermute(value, axis, [(i, i ^ bit) for i in range(count)])]
    ppermute x2 -> x1, starting transfers between devices: 9.49 us -> 4.39 us  [shift(): lax.ppermute(value, axis, [(i, i + steps) for i in range(count - steps)])]
    dot_general x1, matrix products: 2.99 us -> 5.71 us  [body(): jnp.dot(normed, w_key, preferred_element_type=jnp.float32)]
    dot_general x1, matrix products: 5.71 us -> 2.99 us  [body(): jnp.dot(normed, value_weight, preferred_element_type=jnp.float32)]
  transfers between devices with their start and end apart: 38 -> 32, of which waited for: 12 -> 11; matrix products, arithmetic and copies ran while one was open for 10% -> 17% of each run, Pallas kernels for 20% -> 30%
where the time goes in v3:
time: 202 us
  waiting for transfers between devices  66.4 us (33%)
  Pallas kernels  65 us (32%)
  starting transfers between devices  28 us (14%)
  other arithmetic  19.5 us (10%)
  matrix products  15.5 us (8%)
  local copies, waits for them, and re-layouts  6.09 us (3%)
    ppermute x22, waiting for transfers between devices, swap(): return lax.ppermute(value, axis, [(i, i ^ bit) for i in range(count)])  32.9 us
    ppermute x9, waiting for transfers between devices, rotate(): lax.ppermute(value, axis, [(i, (i + steps) % count) for i in range(count)])  31.3 us
    pallas_call x2, Pallas kernels, project(): pl.pallas_call(functools.partial(project_kernel, turns=turns, slots=slots...  17.9 us
    pallas_call x2, Pallas kernels, grad_terms(): pl.pallas_call(functools.partial(terms_kernel, steps=steps), grid_spec=pl...  15.9 us
    ppermute x22, starting transfers between devices, swap(): return lax.ppermute(value, axis, [(i, i ^ bit) for i in range(count)])  15.5 us
    pallas_call x2, Pallas kernels, attention(): pl.pallas_call(functools.partial(attention_kernel, block=block, group=gro...  14 us
    pallas_call x1, Pallas kernels, lead_blocks(): pl.pallas_call(functools.partial(lead_kernel, steps=count, wide=wide), gr...  8.54 us
    ppermute x9, starting transfers between devices, rotate(): lax.ppermute(value, axis, [(i, (i + steps) % count) for i in range(count)])  8.15 us
  transfers between devices with their start and end apart: 32, of which 11 were waited for; matrix products, arithmetic and copies ran while one was open for 17% of the time, Pallas kernels for 30%

profile of v3, /device:TPU:0, one launch (start us, length us, event | category | flops | bytes accessed | tf_op | source)
XLA Modules:
  0.0 201.7 jit_solution(9780957189280903804)
XLA Ops:
  0.8 2.0 %fusion.6 = (bf16[128,1408]{1,0:T(8,128)(2,1)S(1)}, bf16[128,1408]{1,0:T(8,128)(2,1)S(1)}, bf16[128,1408]{1,0:T(8,128)(2,1)S(1)}) fusion(bf16[1024,5376]{1,0:T(8,128)(2,1)} %w_ref.1, s32[]{:T(128)S(6)} %select_n.87, s32[]{:T(128)S(6)} %select_n.99, s32[]{:T(128)S(6)} %select_n.95, s32[]{:T(128)S(6)} %select_n.91), kind=kLoop, calls=%fused_computation.39 | loop fusion | bytes 2162704 | tf_op jit(solution)/shard_map/dynamic_slice | solution.py:419
  2.8 3.1 %collective-permute-start.1 = (bf16[128,1408]{1,0:T(8,128)(2,1)S(1)}, bf16[128,1408]{1,0:T(8,128)(2,1)S(1)}, u32[]{:S(2)}, u32[]{:S(2)}) collective-permute-start(bf16[128,1408]{1,0:T(8,128)(2,1)S(1)} %get-tuple-element.55), channel_id=1, source_target_pairs={{0,1},{1,2},{2,3},{3,0},{4,5},{5,6},{6,7},{7,4},{8,9},{9,10},{10,1... | collective-permute-start | bytes 1081352 | tf_op jit(solution)/shard_map/ppermute | solution.py:31
  5.9 2.6 %collective-permute-start.2 = (bf16[128,1408]{1,0:T(8,128)(2,1)S(1)}, bf16[128,1408]{1,0:T(8,128)(2,1)}, u32[]{:S(2)}, u32[]{:S(2)}) collective-permute-start(bf16[128,1408]{1,0:T(8,128)(2,1)S(1)} %get-tuple-element.54), channel_id=1, source_target_pairs={{0,2},{1,3},{2,0},{3,1},{4,6},{5,7},{6,4},{7,5},{8,10},{9,11},{10,... | collective-permute-start | bytes 1081352 | tf_op jit(solution)/shard_map/ppermute | solution.py:31
  10.6 3.9 %fusion = f32[512]{0:T(512)S(1)} fusion(bf16[512,5376]{1,0:T(8,128)(2,1)} %param.13), kind=kLoop, calls=%fused_computation.2 | loop fusion | flops 8257024 | bytes 5507072 | tf_op jit(solution)/shard_map/reduce_sum | solution.py:424
  16.4 3.0 %convolution_convert_fusion.1 = bf16[512,512]{1,0:T(8,128)(2,1)S(1)} fusion(bf16[512,5376]{1,0:T(8,128)(2,1)S(1)} %fusion.2, bf16[5376,512]{1,0:T(8,128)(2,1)S(1)} %bitcast.27), kind=kOutput, calls=%fused_computation.6 | convolution fusion | flops 2818834432 | bytes 11534336 | tf_op jit(solution)/shard_map/dot_general | solution.py:429
  19.4 5.7 %convolution_convert_fusion.2 = bf16[512,512]{1,0:T(8,128)(2,1)S(1)} fusion(bf16[512,5376]{1,0:T(8,128)(2,1)S(1)} %fusion.2, bf16[5376,512]{1,0:T(8,128)(2,1)} %param.16), kind=kOutput, calls=%fused_computation.7 | convolution fusion | flops 2818834432 | bytes 11534336 | tf_op jit(solution)/shard_map/dot_general | solution.py:428
  25.3 4.4 %collective-permute-start = (bf16[512,1024]{1,0:T(8,128)(2,1)S(1)}, bf16[512,1024]{1,0:T(8,128)(2,1)}, u32[]{:S(2)}, u32[]{:S(2)}) collective-permute-start(bf16[512,1024]{1,0:T(8,128)(2,1)S(1)} %pad_maximum_fusion.1.k0_ref.v0_ref), channel_id=1, source_target_pairs={{0,8},{4,12},{8,16},{12,20},{16,24},{20,28},{1,9},{5,13},{9,17},{1... | collective-permute-start | bytes 3145736 | tf_op jit(solution)/shard_map/ppermute | solution.py:26
  29.7 6.8 %convolution_convert_fusion.q_ref = bf16[512,1024]{1,0:T(8,128)(2,1)} fusion(bf16[512,5376]{1,0:T(8,128)(2,1)S(1)} %fusion.2, bf16[5376,1024]{1,0:T(8,128)(2,1)S(1)} %bitcast.25), kind=kOutput, calls=%fused_computation.5 | convolution fusion | flops 5637668864 | bytes 17563648 | tf_op jit(solution)/shard_map/dot_general | solution.py:433
  39.6 8.5 %lead.1 = (bf16[4,672,512]{2,1,0:T(8,128)(2,1)}, bf16[4,672,512]{2,1,0:T(8,128)(2,1)}) custom-call(s32[16]{0:T(128)} %pad_add_fusion.tab_ref, bf16[512,5376]{1,0:T(8,128)(2,1)} %cot_ref.1), custom_call_target="tpu_custom_call" | custom-call | flops 22020096 | bytes 11010048 | tf_op jit(solution)/shard_map/lead/pallas_call | solution.py:178
  48.1 2.2 %collective-permute-done.k2_ref.v2_ref = bf16[512,1024]{1,0:T(8,128)(2,1)} collective-permute-done((bf16[512,1024]{1,0:T(8,128)(2,1)S(1)}, bf16[512,1024]{1,0:T(8,128)(2,1)}, u32[]{:S(2)}, u32[]{:S(2)}) %collective-permute-start) | collective-permute-done | bytes 1048608 | tf_op jit(solution)/shard_map/ppermute | solution.py:26
  50.7 2.7 %collective-permute-start.11 = (bf16[3,128,1408]{2,1,0:T(8,128)(2,1)S(1)}, bf16[3,128,1408]{2,1,0:T(8,128)(2,1)S(1)}, u32[]{:S(2)}, u32[]{:S(2)}) collective-permute-start(bf16[3,128,1408]{2,1,0:T(8,128)(2,1)S(1)} %pad_maximum_fusion.refs_5_), channel_id=1, source_target_pairs={{0,8},{4,12},{8,0},{12,4},{16,24},{20,28},{24,16},{28,20},{1,9},{5... | collective-permute-start | bytes 3244040 | tf_op jit(solution)/shard_map/ppermute | solution.py:36
  56.0 7.0 %attention.3 = (bf16[512,512]{1,0:T(8,128)(2,1)}, bf16[512,512]{1,0:T(8,128)(2,1)}) custom-call(s32[1]{0:T(128)} %bitcast.pos_ref, bf16[512,1024]{1,0:T(8,128)(2,1)} %convolution_convert_fusion.q_ref, bf16[512,1024]{1,0:T(8,128)(2,1)} %collective-permute-done.k2_ref.v2_ref, bf16[512,1024]{1,0:T(8,128)(2,1)} %copy-done.15, bf16[512,1024]{1,0:T(8,128)(2,1)} %copy-done.6, ...), custom_call_target="tpu_custom_call" | custom-call | flops 2684354560 | bytes 2621440 | tf_op jit(solution)/shard_map/attention/pallas_call | solution.py:135
  63.6 14.2 %collective-permute-done.11.refs_6_ = bf16[3,128,1408]{2,1,0:T(8,128)(2,1)S(1)} collective-permute-done((bf16[3,128,1408]{2,1,0:T(8,128)(2,1)S(1)}, bf16[3,128,1408]{2,1,0:T(8,128)(2,1)S(1)}, u32[]{:S(2)}, u32[]{:S(2)}) %collective-permute-start.11) | collective-permute-done | bytes 1081376 | tf_op jit(solution)/shard_map/ppermute | solution.py:36
  77.8 2.7 %collective-permute-start.13 = (bf16[3,128,1408]{2,1,0:T(8,128)(2,1)S(1)}, bf16[3,128,1408]{2,1,0:T(8,128)(2,1)}, u32[]{:S(2)}, u32[]{:S(2)}) collective-permute-start(bf16[3,128,1408]{2,1,0:T(8,128)(2,1)S(1)} %collective-permute-done.11.refs_6_), channel_id=1, source_target_pairs={{0,16},{4,20},{8,24},{12,28},{16,0},{20,4},{24,8},{28,12},{1,17},{... | collective-permute-start | bytes 3244040 | tf_op jit(solution)/shard_map/ppermute | solution.py:36
  80.5 7.0 %attention.2 = (bf16[512,512]{1,0:T(8,128)(2,1)}, bf16[512,512]{1,0:T(8,128)(2,1)}) custom-call(s32[1]{0:T(128)} %bitcast.pos_ref, bf16[512,1024]{1,0:T(8,128)(2,1)} %convolution_convert_fusion.q_ref, bf16[512,1024]{1,0:T(8,128)(2,1)} %collective-permute-done.k2_ref.v2_ref, bf16[512,1024]{1,0:T(8,128)(2,1)} %copy-done.15, bf16[512,1024]{1,0:T(8,128)(2,1)} %copy-done.6, ...), custom_call_target="tpu_custom_call" | custom-call | flops 2684354560 | bytes 2621440 | tf_op jit(solution)/shard_map/attention/pallas_call | solution.py:135
  89.3 7.9 %grad_terms.3 = (bf16[2,672,256]{2,1,0:T(8,128)(2,1)}, bf16[2,672,256]{2,1,0:T(8,128)(2,1)}, bf16[2,672,256]{2,1,0:T(8,128)(2,1)}, bf16[2,672,256]{2,1,0:T(8,128)(2,1)}) custom-call(s32[28]{0:T(128)} %pad_add_fusion.1.tab_ref, bf16[4,672,512]{2,1,0:T(8,128)(2,1)} %get-tuple-element.31.cot0_ref, bf16[4,672,512]{2,1,0:T(8,128)(2,1)} %collective-permute-done.18.cot1_ref, ...), custom_call_target="tpu_custom_call" | custom-call | flops 2818572288 | bytes 8257536 | tf_op jit(solution)/shard_map/grad_terms/pallas_call | solution.py:238
  97.7 6.8 %collective-permute-done.7.refs_3_ = bf16[512,512]{1,0:T(8,128)(2,1)} collective-permute-done((bf16[512,512]{1,0:T(8,128)(2,1)}, bf16[512,512]{1,0:T(8,128)(2,1)}, u32[]{:S(2)}, u32[]{:S(2)}) %collective-permute-start.7) | collective-permute-done | bytes 524320 | tf_op jit(solution)/shard_map/ppermute | solution.py:31
  104.5 11.2 %collective-permute-done.5.refs_2_ = bf16[512,512]{1,0:T(8,128)(2,1)} collective-permute-done((bf16[512,512]{1,0:T(8,128)(2,1)}, bf16[512,512]{1,0:T(8,128)(2,1)}, u32[]{:S(2)}, u32[]{:S(2)}) %collective-permute-start.5) | collective-permute-done | bytes 524320 | tf_op jit(solution)/shard_map/ppermute | solution.py:31
  116.3 7.9 %grad_terms.2 = (bf16[2,672,256]{2,1,0:T(8,128)(2,1)}, bf16[2,672,256]{2,1,0:T(8,128)(2,1)}, bf16[2,672,256]{2,1,0:T(8,128)(2,1)}, bf16[2,672,256]{2,1,0:T(8,128)(2,1)}) custom-call(s32[28]{0:T(128)} %pad_add_fusion.1.tab_ref, bf16[4,672,512]{2,1,0:T(8,128)(2,1)} %get-tuple-element.31.cot0_ref, bf16[4,672,512]{2,1,0:T(8,128)(2,1)} %collective-permute-done.18.cot1_ref, ...), custom_call_target="tpu_custom_call" | custom-call | flops 2818572288 | bytes 8257536 | tf_op jit(solution)/shard_map/grad_terms/pallas_call | solution.py:238
  124.9 2.1 %collective-permute-done.8.refs_1_ = bf16[512,512]{1,0:T(8,128)(2,1)} collective-permute-done((bf16[512,512]{1,0:T(8,128)(2,1)}, bf16[512,512]{1,0:T(8,128)(2,1)}, u32[]{:S(2)}, u32[]{:S(2)}) %collective-permute-start.8) | collective-permute-done | bytes 524320 | tf_op jit(solution)/shard_map/ppermute | solution.py:31
  127.0 10.7 %collective-permute-done.6.refs_0_ = bf16[512,512]{1,0:T(8,128)(2,1)} collective-permute-done((bf16[512,512]{1,0:T(8,128)(2,1)}, bf16[512,512]{1,0:T(8,128)(2,1)}, u32[]{:S(2)}, u32[]{:S(2)}) %collective-permute-start.6) | collective-permute-done | bytes 524320 | tf_op jit(solution)/shard_map/ppermute | solution.py:31
  139.4 3.7 %turned.1.refs_12_ = bf16[672,1024]{1,0:T(8,128)(2,1)} custom-call(s32[5]{0:T(128)} %stack.35.pos_ref, bf16[1024,5376]{1,0:T(8,128)(2,1)} %w_ref.1), custom_call_target="tpu_custom_call" | custom-call | tf_op jit(solution)/shard_map/turned/pallas_call | solution.py:385
  143.8 1.9 add_convert_fusion
  145.7 1.9 add_convert_fusion.1
  147.6 1.9 add_convert_fusion.2
  149.5 11.4 %collective-permute-done.20.refs_1_ = bf16[2,672,256]{2,1,0:T(8,128)(2,1)S(1)} collective-permute-done((bf16[2,672,256]{2,1,0:T(8,128)(2,1)}, bf16[2,672,256]{2,1,0:T(8,128)(2,1)S(1)}, u32[]{:S(2)}, u32[]{:S(2)}) %collective-permute-start.20) | collective-permute-done | bytes 688160 | tf_op jit(solution)/shard_map/ppermute | solution.py:36
  160.8 2.0 %add_convert_fusion.3 = bf16[1,672,256]{2,1,0:T(8,128)(2,1)} fusion(bf16[2,672,256]{2,1,0:T(8,128)(2,1)S(1)} %collective-permute-done.20.refs_1_, bf16[2,672,256]{2,1,0:T(8,128)(2,1)} %get-tuple-element.37.refs_0_), kind=kLoop, calls=%fused_computation.14 | loop fusion | flops 688128 | bytes 1032192 | tf_op jit(solution)/shard_map/convert_element_type | solution.py:484
  167.0 8.7 %project.2.refs_4_ = f32[512,1408]{1,0:T(8,128)} custom-call(s32[5]{0:T(128)} %stack.35.pos_ref, bf16[512,512]{1,0:T(8,128)(2,1)} %get-tuple-element.33.refs_0_, bf16[512,512]{1,0:T(8,128)(2,1)} %get-tuple-element.34.refs_1_, bf16[512,512]{1,0:T(8,128)(2,1)} %collective-permute-done.5.refs_2_, bf16[512,512]{1,0:T(8,128)(2,1)} %collective-permute-done.7.refs_3_, ...), custom_call_target="tpu_custom_call" | custom-call | flops 2952790016 | bytes 13631488 | tf_op jit(solution)/shard_map/project/pallas_call | solution.py:310
  176.1 9.2 %project.3 = bf16[1344,512]{1,0:T(8,128)(2,1)} custom-call(s32[5]{0:T(128)} %stack.35.pos_ref, bf16[512,512]{1,0:T(8,128)(2,1)} %collective-permute-done.6.refs_0_, bf16[512,512]{1,0:T(8,128)(2,1)} %collective-permute-done.8.refs_1_, bf16[512,512]{1,0:T(8,128)(2,1)} %collective-permute-done.9.refs_2_, bf16[512,512]{1,0:T(8,128)(2,1)} %collective-permute-done.10.refs_3_, ...), custom_call_target="tpu_custom_call" | custom-call | flops 2952790016 | bytes 13631488 | tf_op jit(solution)/shard_map/project/pallas_call | solution.py:310
  187.1 4.9 %finish.1 = (f32[672,1024]{1,0:T(8,128)}, f32[1,1024]{1,0:T(1,128)}) custom-call(bf16[2,672,256]{2,1,0:T(8,128)(2,1)} %get-tuple-element.37.refs_0_, bf16[2,672,256]{2,1,0:T(8,128)(2,1)} %copy-done.5, bf16[1,672,256]{2,1,0:T(8,128)(2,1)} %copy-done.11, bf16[2,672,256]{2,1,0:T(8,128)(2,1)} %get-tuple-element.39.refs_3_, ...), custom_call_target="tpu_custom_call" | custom-call | flops 5505024 | bytes 8257536 | tf_op jit(solution)/shard_map/finish/pallas_call | solution.py:356
  194.6 3.0 %collective-permute-done.30 = f32[8]{0:T(128)S(1)} collective-permute-done((f32[8]{0:T(128)S(1)}, f32[8]{0:T(128)S(1)}, u32[]{:S(2)}, u32[]{:S(2)}) %collective-permute-start.30) | collective-permute-done | bytes 64 | tf_op jit(solution)/shard_map/ppermute | solution.py:36
  198.0 3.2 %collective-permute-done.31 = f32[8]{0:T(128)S(1)} collective-permute-done((f32[8]{0:T(128)S(1)}, f32[8]{0:T(128)S(1)}, u32[]{:S(2)}, u32[]{:S(2)}) %collective-permute-start.31) | collective-permute-done | bytes 64 | tf_op jit(solution)/shard_map/ppermute | solution.py:36
  (117 shorter events, 26.2 us)
Async XLA Ops:
  2.8 33.7 %collective-permute-start.1 = (bf16[128,1408]{1,0:T(8,128)(2,1)S(1)}, bf16[128,1408]{1,0:T(8,128)(2,1)S(1)}, u32[]{:S(2)}, u32[]{:S(2)}) collective-permute-start(bf16[128,1408]{1,0:T(8,128)(2,1)S(1)} %get-tuple-element.55), channel_id=1, source_target_pairs={{0,1},{1,2},{2,3},{3,0},{4,5},{5,6},{6,7},{7,4},{8,9},{9,10},{10,1... | collective-permute-start | bytes 1081352 | tf_op jit(solution)/shard_map/ppermute | solution.py:31
  5.9 30.6 %collective-permute-start.2 = (bf16[128,1408]{1,0:T(8,128)(2,1)S(1)}, bf16[128,1408]{1,0:T(8,128)(2,1)}, u32[]{:S(2)}, u32[]{:S(2)}) collective-permute-start(bf16[128,1408]{1,0:T(8,128)(2,1)S(1)} %get-tuple-element.54), channel_id=1, source_target_pairs={{0,2},{1,3},{2,0},{3,1},{4,6},{5,7},{6,4},{7,5},{8,10},{9,11},{10,... | collective-permute-start | bytes 1081352 | tf_op jit(solution)/shard_map/ppermute | solution.py:31
  8.5 28.0 %collective-permute-start.3 = (bf16[128,1408]{1,0:T(8,128)(2,1)S(1)}, bf16[128,1408]{1,0:T(8,128)(2,1)}, u32[]{:S(2)}, u32[]{:S(2)}) collective-permute-start(bf16[128,1408]{1,0:T(8,128)(2,1)S(1)} %get-tuple-element.53), channel_id=1, source_target_pairs={{0,3},{1,0},{2,1},{3,2},{4,7},{5,4},{6,5},{7,6},{8,11},{9,8},{10,9... | collective-permute-start | bytes 1081352 | tf_op jit(solution)/shard_map/ppermute | solution.py:31
  25.3 25.0 %collective-permute-start = (bf16[512,1024]{1,0:T(8,128)(2,1)S(1)}, bf16[512,1024]{1,0:T(8,128)(2,1)}, u32[]{:S(2)}, u32[]{:S(2)}) collective-permute-start(bf16[512,1024]{1,0:T(8,128)(2,1)S(1)} %pad_maximum_fusion.1.k0_ref.v0_ref), channel_id=1, source_target_pairs={{0,8},{4,12},{8,16},{12,20},{16,24},{20,28},{1,9},{5,13},{9,17},{1... | collective-permute-start | bytes 3145736 | tf_op jit(solution)/shard_map/ppermute | solution.py:26
  48.1 40.2 %collective-permute-start.18 = (bf16[4,672,512]{2,1,0:T(8,128)(2,1)}, bf16[4,672,512]{2,1,0:T(8,128)(2,1)}, u32[]{:S(2)}, u32[]{:S(2)}) collective-permute-start(bf16[4,672,512]{2,1,0:T(8,128)(2,1)} %get-tuple-element.35), channel_id=1, source_target_pairs={{0,4},{4,0},{8,12},{12,8},{16,20},{20,16},{24,28},{28,24},{1,5},{5... | collective-permute-start | bytes 8257544 | tf_op jit(solution)/shard_map/ppermute | solution.py:36
  50.6 4.3 %collective-permute-start.4 = (bf16[512,1024]{1,0:T(8,128)(2,1)S(1)}, bf16[512,1024]{1,0:T(8,128)(2,1)S(1)}, u32[]{:S(2)}, u32[]{:S(2)}) collective-permute-start(bf16[512,1024]{1,0:T(8,128)(2,1)S(1)} %broadcast_select_fusion), channel_id=1, source_target_pairs={{0,4},{4,0},{8,12},{12,8},{16,20},{20,16},{24,28},{28,24},{1,5},{5... | collective-permute-start | bytes 3145736 | tf_op jit(solution)/shard_map/ppermute | solution.py:36
  50.7 27.1 %collective-permute-start.11 = (bf16[3,128,1408]{2,1,0:T(8,128)(2,1)S(1)}, bf16[3,128,1408]{2,1,0:T(8,128)(2,1)S(1)}, u32[]{:S(2)}, u32[]{:S(2)}) collective-permute-start(bf16[3,128,1408]{2,1,0:T(8,128)(2,1)S(1)} %pad_maximum_fusion.refs_5_), channel_id=1, source_target_pairs={{0,8},{4,12},{8,0},{12,4},{16,24},{20,28},{24,16},{28,20},{1,9},{5... | collective-permute-start | bytes 3244040 | tf_op jit(solution)/shard_map/ppermute | solution.py:36
  53.3 34.1 %collective-permute-start.12 = (bf16[3,128,1408]{2,1,0:T(8,128)(2,1)S(1)}, bf16[3,128,1408]{2,1,0:T(8,128)(2,1)S(1)}, u32[]{:S(2)}, u32[]{:S(2)}) collective-permute-start(bf16[3,128,1408]{2,1,0:T(8,128)(2,1)S(1)} %pad_maximum_fusion.refs_5_), channel_id=1, source_target_pairs={{0,16},{4,20},{8,24},{12,28},{16,0},{20,4},{24,8},{28,12},{1,17},{... | collective-permute-start | bytes 3244040 | tf_op jit(solution)/shard_map/ppermute | solution.py:36
  54.9 42.4 %collective-permute-start.14 = (bf16[3,128,1408]{2,1,0:T(8,128)(2,1)S(1)}, bf16[3,128,1408]{2,1,0:T(8,128)(2,1)}, u32[]{:S(2)}, u32[]{:S(2)}) collective-permute-start(bf16[3,128,1408]{2,1,0:T(8,128)(2,1)S(1)} %pad_maximum_fusion.refs_5_), channel_id=1, source_target_pairs={{0,4},{4,0},{8,12},{12,8},{16,20},{20,16},{24,28},{28,24},{1,5},{5... | collective-permute-start | bytes 3244040 | tf_op jit(solution)/shard_map/ppermute | solution.py:36
  63.0 24.6 %collective-permute-start.24 = (bf16[512,512]{1,0:T(8,128)(2,1)}, bf16[512,512]{1,0:T(8,128)(2,1)}, u32[]{:S(2)}, u32[]{:S(2)}) collective-permute-start(bf16[512,512]{1,0:T(8,128)(2,1)} %get-tuple-element.41.att0_ref), channel_id=1, source_target_pairs={{0,4},{4,0},{8,12},{12,8},{16,20},{20,16},{24,28},{28,24},{1,5},{5... | collective-permute-start | bytes 1572872 | tf_op jit(solution)/shard_map/ppermute | solution.py:36
  77.8 46.5 %collective-permute-start.13 = (bf16[3,128,1408]{2,1,0:T(8,128)(2,1)S(1)}, bf16[3,128,1408]{2,1,0:T(8,128)(2,1)}, u32[]{:S(2)}, u32[]{:S(2)}) collective-permute-start(bf16[3,128,1408]{2,1,0:T(8,128)(2,1)S(1)} %collective-permute-done.11.refs_6_), channel_id=1, source_target_pairs={{0,16},{4,20},{8,24},{12,28},{16,0},{20,4},{24,8},{28,12},{1,17},{... | collective-permute-start | bytes 3244040 | tf_op jit(solution)/shard_map/ppermute | solution.py:36
  87.5 28.3 %collective-permute-start.19 = (bf16[512,512]{1,0:T(8,128)(2,1)}, bf16[512,512]{1,0:T(8,128)(2,1)}, u32[]{:S(2)}, u32[]{:S(2)}) collective-permute-start(bf16[512,512]{1,0:T(8,128)(2,1)} %get-tuple-element.36.att0_ref), channel_id=1, source_target_pairs={{0,4},{4,0},{8,12},{12,8},{16,20},{20,16},{24,28},{28,24},{1,5},{5... | collective-permute-start | bytes 1572872 | tf_op jit(solution)/shard_map/ppermute | solution.py:36
  87.6 17.0 %collective-permute-start.7 = (bf16[512,512]{1,0:T(8,128)(2,1)}, bf16[512,512]{1,0:T(8,128)(2,1)}, u32[]{:S(2)}, u32[]{:S(2)}) collective-permute-start(bf16[512,512]{1,0:T(8,128)(2,1)} %get-tuple-element.34.refs_1_), channel_id=1, source_target_pairs={{0,1},{1,2},{2,3},{3,0},{4,5},{5,6},{6,7},{7,4},{8,9},{9,10},{10,1... | collective-permute-start | bytes 1572872 | tf_op jit(solution)/shard_map/ppermute | solution.py:31
  88.3 27.4 %collective-permute-start.5 = (bf16[512,512]{1,0:T(8,128)(2,1)}, bf16[512,512]{1,0:T(8,128)(2,1)}, u32[]{:S(2)}, u32[]{:S(2)}) collective-permute-start(bf16[512,512]{1,0:T(8,128)(2,1)} %get-tuple-element.33.refs_0_), channel_id=1, source_target_pairs={{0,1},{1,2},{2,3},{3,0},{4,5},{5,6},{6,7},{7,4},{8,9},{9,10},{10,1... | collective-permute-start | bytes 1572872 | tf_op jit(solution)/shard_map/ppermute | solution.py:31
  97.3 40.4 %collective-permute-start.27 = (bf16[2,672,256]{2,1,0:T(8,128)(2,1)}, bf16[2,672,256]{2,1,0:T(8,128)(2,1)}, u32[]{:S(2)}, u32[]{:S(2)}) collective-permute-start(bf16[2,672,256]{2,1,0:T(8,128)(2,1)} %get-tuple-element.45), channel_id=1, source_target_pairs={{0,16},{4,20},{8,24},{12,28},{16,0},{20,4},{24,8},{28,12},{1,17},{... | collective-permute-start | bytes 2064392 | tf_op jit(solution)/shard_map/ppermute | solution.py:36
  104.5 22.5 %collective-permute-start.8 = (bf16[512,512]{1,0:T(8,128)(2,1)}, bf16[512,512]{1,0:T(8,128)(2,1)}, u32[]{:S(2)}, u32[]{:S(2)}) collective-permute-start(bf16[512,512]{1,0:T(8,128)(2,1)} %collective-permute-done.7.refs_3_), channel_id=1, source_target_pairs={{0,1},{1,2},{2,3},{3,0},{4,5},{5,6},{6,7},{7,4},{8,9},{9,10},{10,1... | collective-permute-start | bytes 1572872 | tf_op jit(solution)/shard_map/ppermute | solution.py:31
  115.8 21.9 %collective-permute-start.6 = (bf16[512,512]{1,0:T(8,128)(2,1)}, bf16[512,512]{1,0:T(8,128)(2,1)}, u32[]{:S(2)}, u32[]{:S(2)}) collective-permute-start(bf16[512,512]{1,0:T(8,128)(2,1)} %collective-permute-done.5.refs_2_), channel_id=1, source_target_pairs={{0,1},{1,2},{2,3},{3,0},{4,5},{5,6},{6,7},{7,4},{8,9},{9,10},{10,1... | collective-permute-start | bytes 1572872 | tf_op jit(solution)/shard_map/ppermute | solution.py:31
  115.8 27.4 %collective-permute-start.25 = (bf16[2,672,256]{2,1,0:T(8,128)(2,1)}, bf16[2,672,256]{2,1,0:T(8,128)(2,1)}, u32[]{:S(2)}, u32[]{:S(2)}) collective-permute-start(bf16[2,672,256]{2,1,0:T(8,128)(2,1)} %get-tuple-element.43), channel_id=1, source_target_pairs={{0,8},{4,12},{8,0},{12,4},{16,24},{20,28},{24,16},{28,20},{1,9},{5... | collective-permute-start | bytes 2064392 | tf_op jit(solution)/shard_map/ppermute | solution.py:36
  124.3 21.4 %collective-permute-start.22 = (bf16[2,672,256]{2,1,0:T(8,128)(2,1)}, bf16[2,672,256]{2,1,0:T(8,128)(2,1)}, u32[]{:S(2)}, u32[]{:S(2)}) collective-permute-start(bf16[2,672,256]{2,1,0:T(8,128)(2,1)} %get-tuple-element.40), channel_id=1, source_target_pairs={{0,16},{4,20},{8,24},{12,28},{16,0},{20,4},{24,8},{28,12},{1,17},{... | collective-permute-start | bytes 2064392 | tf_op jit(solution)/shard_map/ppermute | solution.py:36
  127.0 35.9 %collective-permute-start.15 = (bf16[3,128,1408]{2,1,0:T(8,128)(2,1)S(1)}, bf16[3,128,1408]{2,1,0:T(8,128)(2,1)S(1)}, u32[]{:S(2)}, u32[]{:S(2)}) collective-permute-start(bf16[3,128,1408]{2,1,0:T(8,128)(2,1)S(1)} %collective-permute-done.11.refs_6_), channel_id=1, source_target_pairs={{0,4},{4,0},{8,12},{12,8},{16,20},{20,16},{24,28},{28,24},{1,5},{5... | collective-permute-start | bytes 3244040 | tf_op jit(solution)/shard_map/ppermute | solution.py:36
  137.7 25.8 %collective-permute-start.16 = (bf16[3,128,1408]{2,1,0:T(8,128)(2,1)S(1)}, bf16[3,128,1408]{2,1,0:T(8,128)(2,1)}, u32[]{:S(2)}, u32[]{:S(2)}) collective-permute-start(bf16[3,128,1408]{2,1,0:T(8,128)(2,1)S(1)} %collective-permute-done.12.refs_7_), channel_id=1, source_target_pairs={{0,4},{4,0},{8,12},{12,8},{16,20},{20,16},{24,28},{28,24},{1,5},{5... | collective-permute-start | bytes 3244040 | tf_op jit(solution)/shard_map/ppermute | solution.py:36
  137.7 26.3 %collective-permute-start.17 = (bf16[3,128,1408]{2,1,0:T(8,128)(2,1)}, bf16[3,128,1408]{2,1,0:T(8,128)(2,1)}, u32[]{:S(2)}, u32[]{:S(2)}) collective-permute-start(bf16[3,128,1408]{2,1,0:T(8,128)(2,1)} %collective-permute-done.13.refs_8_), channel_id=1, source_target_pairs={{0,4},{4,0},{8,12},{12,8},{16,20},{20,16},{24,28},{28,24},{1,5},{5... | collective-permute-start | bytes 3244040 | tf_op jit(solution)/shard_map/ppermute | solution.py:36
  143.2 17.7 %collective-permute-start.20 = (bf16[2,672,256]{2,1,0:T(8,128)(2,1)}, bf16[2,672,256]{2,1,0:T(8,128)(2,1)S(1)}, u32[]{:S(2)}, u32[]{:S(2)}) collective-permute-start(bf16[2,672,256]{2,1,0:T(8,128)(2,1)} %get-tuple-element.38), channel_id=1, source_target_pairs={{0,8},{4,12},{8,0},{12,4},{16,24},{20,28},{24,16},{28,20},{1,9},{5... | collective-permute-start | bytes 2064392 | tf_op jit(solution)/shard_map/ppermute | solution.py:36
  145.7 19.6 %collective-permute-start.10 = (bf16[512,512]{1,0:T(8,128)(2,1)}, bf16[512,512]{1,0:T(8,128)(2,1)}, u32[]{:S(2)}, u32[]{:S(2)}) collective-permute-start(bf16[512,512]{1,0:T(8,128)(2,1)} %collective-permute-done.8.refs_1_), channel_id=1, source_target_pairs={{0,1},{1,2},{2,3},{3,0},{4,5},{5,6},{6,7},{7,4},{8,9},{9,10},{10,1... | collective-permute-start | bytes 1572872 | tf_op jit(solution)/shard_map/ppermute | solution.py:31
  160.8 15.3 %collective-permute-start.9 = (bf16[512,512]{1,0:T(8,128)(2,1)}, bf16[512,512]{1,0:T(8,128)(2,1)}, u32[]{:S(2)}, u32[]{:S(2)}) collective-permute-start(bf16[512,512]{1,0:T(8,128)(2,1)} %collective-permute-done.6.refs_0_), channel_id=1, source_target_pairs={{0,1},{1,2},{2,3},{3,0},{4,5},{5,6},{6,7},{7,4},{8,9},{9,10},{10,1... | collective-permute-start | bytes 1572872 | tf_op jit(solution)/shard_map/ppermute | solution.py:31
  162.9 22.5 %collective-permute-start.28 = (bf16[1,672,256]{2,1,0:T(8,128)(2,1)}, bf16[1,672,256]{2,1,0:T(8,128)(2,1)S(1)}, u32[]{:S(2)}, u32[]{:S(2)}) collective-permute-start(bf16[1,672,256]{2,1,0:T(8,128)(2,1)} %add_convert_fusion), channel_id=1, source_target_pairs={{0,8},{4,12},{8,0},{12,4},{16,24},{20,28},{24,16},{28,20},{1,9},{5... | collective-permute-start | bytes 1032200 | tf_op jit(solution)/shard_map/ppermute | solution.py:36
  163.5 21.9 %collective-permute-start.26 = (bf16[1,672,256]{2,1,0:T(8,128)(2,1)}, bf16[1,672,256]{2,1,0:T(8,128)(2,1)S(1)}, u32[]{:S(2)}, u32[]{:S(2)}) collective-permute-start(bf16[1,672,256]{2,1,0:T(8,128)(2,1)} %add_convert_fusion.1), channel_id=1, source_target_pairs={{0,16},{4,20},{8,24},{12,28},{16,0},{20,4},{24,8},{28,12},{1,17},{... | collective-permute-start | bytes 1032200 | tf_op jit(solution)/shard_map/ppermute | solution.py:36
  164.0 21.4 %collective-permute-start.23 = (bf16[1,672,256]{2,1,0:T(8,128)(2,1)}, bf16[1,672,256]{2,1,0:T(8,128)(2,1)S(1)}, u32[]{:S(2)}, u32[]{:S(2)}) collective-permute-start(bf16[1,672,256]{2,1,0:T(8,128)(2,1)} %add_convert_fusion.2), channel_id=1, source_target_pairs={{0,8},{4,12},{8,0},{12,4},{16,24},{20,28},{24,16},{28,20},{1,9},{5... | collective-permute-start | bytes 1032200 | tf_op jit(solution)/shard_map/ppermute | solution.py:36
  165.3 20.1 %collective-permute-start.21 = (bf16[1,672,256]{2,1,0:T(8,128)(2,1)}, bf16[1,672,256]{2,1,0:T(8,128)(2,1)S(1)}, u32[]{:S(2)}, u32[]{:S(2)}) collective-permute-start(bf16[1,672,256]{2,1,0:T(8,128)(2,1)} %add_convert_fusion.3), channel_id=1, source_target_pairs={{0,16},{4,20},{8,24},{12,28},{16,0},{20,4},{24,8},{28,12},{1,17},{... | collective-permute-start | bytes 1032200 | tf_op jit(solution)/shard_map/ppermute | solution.py:36
  192.8 1.2 collective-permute-start.29
  194.0 3.6 %collective-permute-start.30 = (f32[8]{0:T(128)S(1)}, f32[8]{0:T(128)S(1)}, u32[]{:S(2)}, u32[]{:S(2)}) collective-permute-start(f32[8]{0:T(128)S(1)} %add.126), channel_id=1, source_target_pairs={{0,8},{4,12},{8,0},{12,4},{16,24},{20,28},{24,16},{28,20},{1,9},{5... | collective-permute-start | bytes 104 | tf_op jit(solution)/shard_map/ppermute | solution.py:36
  197.6 3.6 %collective-permute-start.31 = (f32[8]{0:T(128)S(1)}, f32[8]{0:T(128)S(1)}, u32[]{:S(2)}, u32[]{:S(2)}) collective-permute-start(f32[8]{0:T(128)S(1)} %add.127), channel_id=1, source_target_pairs={{0,16},{4,20},{8,24},{12,28},{16,0},{20,4},{24,8},{28,12},{1,17},{... | collective-permute-start | bytes 104 | tf_op jit(solution)/shard_map/ppermute | solution.py:36
  (23 other events, 321.3 us)
